TPU v7x, 256 devices: a whole 4x4x8 slice. The times are simulated.
256 devices in a mesh: gx: 8 (over z_lo, x), gy: 4 (over z_hi), gz: 8 (over y, core).
Axes of the slice: x: 4, y: 4, z: 8 (z_hi: 4, z_lo: 2; z = z_hi * 2 + z_lo), core: 2. Of those that a mesh axis runs over, the one named last changes fastest.
Arguments:
- displacement: bfloat16 [3, 32, 128, 128], P(None, 'gx', 'gy', 'gz'), may hold values from -6 to 6
- lift_weight: bfloat16 [27, 64, 3], replicated, may hold values from -1 to 1
- encode_weight: bfloat16 [27, 64, 64], replicated, may hold values from -0.21875 to 0.21875
- downward_weight: bfloat16 [8, 128, 64], replicated, may hold values from -0.375 to 0.375
- middle_first: bfloat16 [27, 128, 128], replicated, may hold values from -0.15625 to 0.15625
- middle_second: bfloat16 [27, 128, 128], replicated, may hold values from -0.15625 to 0.15625
- up_weight: bfloat16 [8, 64, 128], replicated, may hold values from -0.75 to 0.75
- decode_weight: bfloat16 [27, 64, 128], replicated, may hold values from -0.15625 to 0.15625
- head_weight: bfloat16 [3, 64], replicated, may hold values from -1 to 1
Outputs:
- imitated: float32 [3, 32, 128, 128], P(None, 'gx', 'gy', 'gz')
All inputs are finite; a program needn't handle non-finite values.
Results may differ from a plain program's by a relative error of at most 0.0055.
Values may be sent and summed in bfloat16 or wider, within the bound.
A program may use at most 64 MiB of HBM per device.

v0:
```python
import jax
import jax.numpy as jnp
import numpy as np
from jax import lax
from jax.experimental import pallas as pl
from jax.experimental.pallas import tpu as pltpu
from jax.sharding import PartitionSpec as P

BF = jnp.bfloat16
F32 = jnp.float32


def act(v):
    return jnp.where(v > 0, v, 0.1 * v)


def lift_selection():
    sel = np.zeros((3, 4, 192, 27), np.float32)
    for oy in range(2):
        for oz in range(2):
            for dx in range(3):
                for dy in range(2):
                    for dz in range(2):
                        for jy in range(2):
                            for jz in range(2):
                                b, c = 2 * dy + jy - oy, 2 * dz + jz - oz
                                if 0 <= b < 3 and 0 <= c < 3:
                                    for ch in range(3):
                                        row = (((dx * 2 + dy) * 2 + dz) * 16 + (jy * 2 + jz) * 3 + ch)
                                        sel[ch, oy * 2 + oz, row, 9 * dx + 3 * b + c] = 1
    return sel.reshape(3, 768, 27)


def dot(a, b):
    return jnp.dot(a, b, preferred_element_type=F32)


def unet(
    qt, lw, sel, ew, dw, m1, m2, uw, cw, hw,
    out,
    patch, wl, we, wd, wm1, wm2, wu, wc, wh,
    f0, f1, skip, coarse, middle, deep, ks, ku, joined,
):
    w = dot(sel[0], lw[0]) + dot(sel[1], lw[1]) + dot(sel[2], lw[2])
    w = w.reshape(4, 192, 64)
    wl[:, 0:128] = jnp.concatenate([w[0], w[1]], axis=1).astype(BF)
    wl[:, 128:256] = jnp.concatenate([w[2], w[3]], axis=1).astype(BF)

    def pair_tiles(src, a, b):
        taps = [src[9 * a + 3 * b + c].astype(F32) for c in range(3)]
        none = jnp.zeros_like(taps[0])
        for m in range(4):
            lo = taps[m] if m < 3 else none
            hi = taps[m - 1] if m > 0 else none
            yield m, jnp.transpose(jnp.concatenate([lo, hi], axis=0)).astype(BF)

    we[...] = jnp.zeros_like(we)
    wc[...] = jnp.zeros_like(wc)
    wm1[...] = jnp.zeros_like(wm1)
    wm2[...] = jnp.zeros_like(wm2)
    for a in range(3):
        for b in range(3):
            for m, tile in pair_tiles(ew, a, b):
                dz, jz = m // 2, m % 2
                for dy in range(2):
                    for jy in range(2):
                        oy = 2 * dy + jy - b
                        if 0 <= oy < 2:
                            row = ((a * 2 + dy) * 2 + dz) * 256 + (jy * 2 + jz) * 64
                            we[row : row + 64, oy * 128 : oy * 128 + 128] = tile
            for m, tile in pair_tiles(cw, a, b):
                dz, jz = m // 2, m % 2
                for dy in range(2):
                    for jy in range(2):
                        oy = 2 * dy + jy - b
                        if 0 <= oy < 2:
                            for s in range(2):
                                row = (((s * 3 + a) * 2 + dy) * 2 + dz) * 256 + (jy * 2 + jz) * 64
                                wc[row : row + 64, oy * 128 : oy * 128 + 128] = tile[s * 64 : s * 64 + 64]
            for c in range(3):
                for src, dst in ((m1, wm1), (m2, wm2)):
                    tile = jnp.transpose(src[9 * a + 3 * b + c].astype(F32)).astype(BF)
                    for dy in range(2):
                        for jy in range(2):
                            oy = 2 * dy + jy - b
                            if 0 <= oy < 2:
                                row = ((a * 2 + dy) * 3 + c) * 256 + jy * 128
                                dst[row : row + 128, oy * 128 : oy * 128 + 128] = tile
    wd[...] = dw[...].reshape(2, 256, 128)
    for a in range(2):
        for b in range(2):
            pairs = jnp.concatenate([uw[4 * a + 2 * b + 1], uw[4 * a + 2 * b]], axis=0).astype(F32)
            wu[a, :, b * 128 : b * 128 + 128] = jnp.transpose(pairs).astype(BF)
    wh[...] = jnp.zeros_like(wh)
    for g in range(4):
        wh[3 * g : 3 * g + 3, 64 * g : 64 * g + 64] = hw[...].astype(F32)

    @pl.loop(0, 20)
    def _(x):
        q = qt[x].astype(F32)
        for dy in range(2):
            for dz in range(2):
                s = dy * 16 + dz
                r = pltpu.roll(q, 384 - s, axis=1) if s else q
                g = dy * 2 + dz
                patch[x, 16 * g : 16 * g + 16, :] = r.astype(BF)

    @pl.loop(0, 18)
    def _(x):
        p = patch[pl.ds(x, 3)].reshape(192, 384)
        v = lax.dot_general(p, wl[...], (((0,), (0,)), ((), ())), preferred_element_type=F32)
        v = act(v)
        f0[x] = v.astype(BF)
        f1[x] = pltpu.roll(v, 383, axis=0).astype(BF)

    @pl.loop(0, 8)
    def _(i):
        for h in range(2):
            x = 2 * i + h
            taps = []
            for a in range(3):
                for dy in range(2):
                    for src in (f0, f1):
                        taps.append(src[x + a, dy * 16 : dy * 16 + 352, :])
            v = dot(jnp.concatenate(taps, axis=1), we[...])
            skip[x] = act(v).astype(BF)

    @pl.loop(0, 8)
    def _(x):
        lhs = jnp.concatenate([skip[2 * x], skip[2 * x + 1]], axis=1)
        v = act(dot(lhs, wd[...].reshape(512, 128)))
        for c in range(3):
            r = pltpu.roll(v, 352 - c, axis=0) if c else v
            r = r.reshape(11, 2, 16, 128)
            coarse[c, x, :, 0:128] = r[:, 0].reshape(176, 128).astype(BF)
            coarse[c, x, :, 128:256] = r[:, 1].reshape(176, 128).astype(BF)

    @pl.loop(0, 3)
    def _(i):
        for h in range(2):
            x = 2 * i + h
            taps = []
            for a in range(3):
                for dy in range(2):
                    for c in range(3):
                        taps.append(coarse[c, x + a, dy * 16 : dy * 16 + 160, :])
            v = act(dot(jnp.concatenate(taps, axis=1), wm1[...]))
            for c in range(3):
                r = pltpu.roll(v, 160 - c, axis=0) if c else v
                middle[c, x] = r.astype(BF)

    @pl.loop(0, 2)
    def _(i):
        for h in range(2):
            x = 2 * i + h
            taps = []
            for a in range(3):
                for dy in range(2):
                    for c in range(3):
                        taps.append(middle[c, x + a, dy * 16 : dy * 16 + 144, :])
            v = act(dot(jnp.concatenate(taps, axis=1), wm2[...]))
            deep[x] = v.astype(BF)

    low = lax.broadcasted_iota(jnp.int32, (17, 16, 128), 2) < 64

    def spread(dst, f, blocks):
        for dz in range(2):
            r = pltpu.roll(blocks, 15, axis=1) if dz else blocks
            r = r[:, 0:8]
            for dy in range(2):
                dst[dy, dz, f] = r[dy : dy + 16].reshape(128, 256).astype(BF)

    @pl.loop(0, 6)
    def _(f):
        v = skip[f + 5].astype(F32).reshape(22, 16, 256)
        halves = []
        for jy in range(2):
            s = v[2 + jy : 19 + jy, :, 128 - 128 * jy : 256 - 128 * jy]
            t = jnp.where(low, pltpu.roll(s, 13, axis=1), pltpu.roll(s, 14, axis=1))
            halves.append(pltpu.roll(t, 64, axis=2))
        spread(ks, f, jnp.concatenate(halves, axis=2))

    @pl.loop(0, 6)
    def _(f):
        xd = (f + 1) // 2
        a = (f + 1) % 2
        d = deep[xd]
        us = []
        for jy in range(2):
            us.append(act(dot(d[:, jy * 128 : jy * 128 + 128], wu[a])).reshape(9, 1, 16, 256))
        u = jnp.concatenate(us, axis=1).reshape(18, 16, 256)
        halves = []
        for jy in range(2):
            s = u[jy : 17 + jy, :, 128 - 128 * jy : 256 - 128 * jy]
            halves.append(jnp.where(low, s, pltpu.roll(s, 15, axis=1)))
        spread(ku, f, jnp.concatenate(halves, axis=2))

    @pl.loop(0, 2)
    def _(i):
        x = 2 * i
        taps = []
        for src in (ks, ku):
            for a in range(3):
                for dy in range(2):
                    for dz in range(2):
                        taps.append(src[dy, dz, pl.ds(x + a, 2)].reshape(256, 256))
        v = act(dot(jnp.concatenate(taps, axis=1), wc[...])).astype(BF)
        for h in range(2):
            j = v[h * 128 : h * 128 + 128]
            out[x + h] = lax.dot_general(
                wh[...].astype(BF), j, (((1,), (1,)), ((), ())), preferred_element_type=F32
            )


def network(qt, lw, ew, dw, m1, m2, uw, cw, hw):
    sel = jnp.asarray(lift_selection(), BF)
    vm = pl.BlockSpec(memory_space=pltpu.VMEM)
    return pl.pallas_call(
        unet,
        out_shape=jax.ShapeDtypeStruct((4, 16, 128), F32),
        in_specs=[vm] * 10,
        out_specs=vm,
        scratch_shapes=[
            pltpu.VMEM((20, 64, 384), BF),
            pltpu.VMEM((192, 256), BF),
            pltpu.VMEM((3072, 256), BF),
            pltpu.VMEM((2, 256, 128), BF),
            pltpu.VMEM((4608, 256), BF),
            pltpu.VMEM((4608, 256), BF),
            pltpu.VMEM((2, 128, 256), BF),
            pltpu.VMEM((6144, 256), BF),
            pltpu.VMEM((16, 256), F32),
            pltpu.VMEM((18, 384, 256), BF),
            pltpu.VMEM((18, 384, 256), BF),
            pltpu.VMEM((16, 352, 256), BF),
            pltpu.VMEM((3, 8, 176, 256), BF),
            pltpu.VMEM((3, 6, 160, 256), BF),
            pltpu.VMEM((4, 144, 256), BF),
            pltpu.VMEM((2, 2, 6, 128, 256), BF),
            pltpu.VMEM((2, 2, 6, 128, 256), BF),
            pltpu.VMEM((8, 128), F32),
        ],
        compiler_params=pltpu.CompilerParams(vmem_limit_bytes=56 * 1024 * 1024),
    )(qt, jnp.transpose(lw, (2, 0, 1)), sel, ew, jnp.transpose(dw, (0, 2, 1)), m1, m2, uw, cw, hw)


def ring(value, axis, step):
    n = lax.axis_size(axis)
    return lax.ppermute(value, axis, [(i, (i + step) % n) for i in range(n)])


def local(d, lw, ew, dw, m1, m2, uw, cw, hw):
    wide = jnp.concatenate(
        [ring(d, "gx", 2), ring(d, "gx", 1), d, ring(d, "gx", -1), ring(d, "gx", -2)], axis=1
    )
    for axis, dim in (("gy", 2), ("gz", 3)):
        size = wide.shape[dim]
        head = lax.slice_in_dim(wide, 0, 8, axis=dim)
        tail = lax.slice_in_dim(wide, size - 8, size, axis=dim)
        wide = jnp.concatenate([ring(tail, axis, 1), wide, ring(head, axis, -1)], axis=dim)
    qt = wide.reshape(3, 20, 24, 2, 16, 2).transpose(1, 3, 5, 0, 2, 4).reshape(20, 12, 384)
    qt = jnp.pad(qt, ((0, 0), (0, 4), (0, 0)))
    head = network(qt, lw, ew, dw, m1, m2, uw, cw, hw)
    head = head[:, :12].reshape(4, 2, 2, 3, 16, 8).transpose(3, 0, 4, 1, 5, 2).reshape(3, 4, 32, 16)
    return d.astype(F32) + head


def solution(mesh):
    placed = (P(None, "gx", "gy", "gz"), P(), P(), P(), P(), P(), P(), P(), P())
    return jax.shard_map(
        local, mesh=mesh, in_specs=placed, out_specs=P(None, "gx", "gy", "gz"), check_vma=False
    )
```

profile of v0, /device:TPU:1, one launch (start us, length us, event | category | flops | bytes accessed | tf_op | source)
XLA Modules:
  0.0 79.1 jit_solution(11740290267633480576)
XLA Ops:
  0.0 3.6 %collective-permute-start = (bf16[3,4,32,16]{2,3,1,0:T(8,128)(2,1)}, bf16[3,4,32,16]{2,3,1,0:T(8,128)(2,1)S(1)}, u32[]{:S(2)}, u32[]{:S(2)}) collective-permute-start(bf16[3,4,32,16]{2,3,1,0:T(8,128)(2,1)} %param.10), channel_id=1, source_target_pairs={{0,64},{32,96},{64,128},{96,160},{128,192},{160,224},{192,0},{224,... | collective-permute-start | bytes 36872 | tf_op jit(solution)/shard_map/ppermute | solution.py:249
  3.6 1.8 %collective-permute-start.2 = (bf16[3,4,32,16]{2,3,1,0:T(8,128)(2,1)}, bf16[3,4,32,16]{2,3,1,0:T(8,128)(2,1)S(1)}, u32[]{:S(2)}, u32[]{:S(2)}) collective-permute-start(bf16[3,4,32,16]{2,3,1,0:T(8,128)(2,1)} %param.10), channel_id=1, source_target_pairs={{0,224},{32,0},{64,32},{96,64},{128,96},{160,128},{192,160},{224,1... | collective-permute-start | bytes 36872 | tf_op jit(solution)/shard_map/ppermute | solution.py:249
  5.3 1.7 %collective-permute-start.3 = (bf16[3,4,32,16]{2,3,1,0:T(8,128)(2,1)}, bf16[3,4,32,16]{2,3,1,0:T(8,128)(2,1)S(1)}, u32[]{:S(2)}, u32[]{:S(2)}) collective-permute-start(bf16[3,4,32,16]{2,3,1,0:T(8,128)(2,1)} %param.10), channel_id=1, source_target_pairs={{0,192},{32,224},{64,0},{96,32},{128,64},{160,96},{192,128},{224,1... | collective-permute-start | bytes 36872 | tf_op jit(solution)/shard_map/ppermute | solution.py:249
  7.0 3.7 %collective-permute-done.1 = bf16[3,4,32,16]{2,3,1,0:T(8,128)(2,1)S(1)} collective-permute-done((bf16[3,4,32,16]{2,3,1,0:T(8,128)(2,1)}, bf16[3,4,32,16]{2,3,1,0:T(8,128)(2,1)S(1)}, u32[]{:S(2)}, u32[]{:S(2)}) %collective-permute-start.1) | collective-permute-done | bytes 12320 | tf_op jit(solution)/shard_map/ppermute | solution.py:249
  10.8 0.8 %constant_dynamic-update-slice_fusion.2 = bf16[3,20,32,16]{2,3,1,0:T(8,128)(2,1)S(1)} fusion(bf16[3,20,32,16]{2,3,1,0:T(8,128)(2,1)S(1)} %constant_dynamic-update-slice_fusion.3, bf16[3,4,32,16]{2,3,1,0:T(8,128)(2,1)} %param.10), kind=kLoop, calls=%fused_computation.5 | loop fusion | bytes 61440
  11.8 3.1 %collective-permute-start.4 = (bf16[3,20,8,16]{2,3,1,0:T(8,128)(2,1)S(1)}, bf16[3,20,8,16]{2,3,1,0:T(8,128)(2,1)S(1)}, u32[]{:S(2)}, u32[]{:S(2)}) collective-permute-start(bf16[3,20,8,16]{2,3,1,0:T(8,128)(2,1)S(1)} %get-tuple-element.7), channel_id=1, source_target_pairs={{0,8},{8,16},{16,24},{24,0},{1,9},{9,17},{17,25},{25,1},{2,10},{10... | collective-permute-start | bytes 46088 | tf_op jit(solution)/shard_map/ppermute | solution.py:249
  14.8 3.1 %collective-permute-start.5 = (bf16[3,20,8,16]{2,3,1,0:T(8,128)(2,1)S(1)}, bf16[3,20,8,16]{2,3,1,0:T(8,128)(2,1)S(1)}, u32[]{:S(2)}, u32[]{:S(2)}) collective-permute-start(bf16[3,20,8,16]{2,3,1,0:T(8,128)(2,1)S(1)} %get-tuple-element.8), channel_id=1, source_target_pairs={{0,24},{8,0},{16,8},{24,16},{1,25},{9,1},{17,9},{25,17},{2,26},{10... | collective-permute-start | bytes 46088 | tf_op jit(solution)/shard_map/ppermute | solution.py:249
  18.0 4.8 %collective-permute-done.4 = bf16[3,20,8,16]{2,3,1,0:T(8,128)(2,1)S(1)} collective-permute-done((bf16[3,20,8,16]{2,3,1,0:T(8,128)(2,1)S(1)}, bf16[3,20,8,16]{2,3,1,0:T(8,128)(2,1)S(1)}, u32[]{:S(2)}, u32[]{:S(2)}) %collective-permute-start.4) | collective-permute-done | bytes 15392 | tf_op jit(solution)/shard_map/ppermute | solution.py:249
  22.8 7.3 %collective-permute-done.5 = bf16[3,20,8,16]{2,3,1,0:T(8,128)(2,1)S(1)} collective-permute-done((bf16[3,20,8,16]{2,3,1,0:T(8,128)(2,1)S(1)}, bf16[3,20,8,16]{2,3,1,0:T(8,128)(2,1)S(1)}, u32[]{:S(2)}, u32[]{:S(2)}) %collective-permute-start.5) | collective-permute-done | bytes 15392 | tf_op jit(solution)/shard_map/ppermute | solution.py:249
  30.1 0.2 pad_maximum_fusion.1
  30.4 2.1 %collective-permute-start.6 = (bf16[3,20,48,8]{2,3,1,0:T(8,128)(2,1)S(1)}, bf16[3,20,48,8]{2,3,1,0:T(8,128)(2,1)S(1)}, u32[]{:S(2)}, u32[]{:S(2)}) collective-permute-start(bf16[3,20,48,8]{2,3,1,0:T(8,128)(2,1)S(1)} %get-tuple-element.5), channel_id=1, source_target_pairs={{0,1},{1,2},{2,3},{3,4},{4,5},{5,6},{6,7},{7,0},{8,9},{9,10},{10,1... | collective-permute-start | bytes 138248 | tf_op jit(solution)/shard_map/ppermute | solution.py:249
  32.5 1.9 %collective-permute-done.6 = bf16[3,20,48,8]{2,3,1,0:T(8,128)(2,1)S(1)} collective-permute-done((bf16[3,20,48,8]{2,3,1,0:T(8,128)(2,1)S(1)}, bf16[3,20,48,8]{2,3,1,0:T(8,128)(2,1)S(1)}, u32[]{:S(2)}, u32[]{:S(2)}) %collective-permute-start.6) | collective-permute-done | bytes 46112 | tf_op jit(solution)/shard_map/ppermute | solution.py:249
  34.4 2.4 %collective-permute-done.7 = bf16[3,20,48,8]{2,3,1,0:T(8,128)(2,1)S(1)} collective-permute-done((bf16[3,20,48,8]{2,3,1,0:T(8,128)(2,1)S(1)}, bf16[3,20,48,8]{2,3,1,0:T(8,128)(2,1)S(1)}, u32[]{:S(2)}, u32[]{:S(2)}) %collective-permute-start.7) | collective-permute-done | bytes 46112 | tf_op jit(solution)/shard_map/ppermute | solution.py:249
  36.8 0.3 pad_maximum_fusion
  37.1 1.3 %copy.20 = bf16[3,20,48,32]{1,3,2,0:T(8,128)(2,1)S(1)} copy(bf16[3,20,48,32]{2,3,1,0:T(8,128)(2,1)S(1)} %pad_maximum_fusion) | data formatting | bytes 368640 | tf_op jit(solution)/shard_map/concatenate | solution.py:260
  38.5 2.8 %copy.26 = bf16[20,2,2,3,24,16]{5,4,3,2,1,0:T(8,128)(2,1)S(1)} copy(bf16[20,2,2,3,24,16]{0,2,5,1,4,3:T(2,128)(2,1)S(1)} %bitcast.12) | data formatting | bytes 368640 | tf_op jit(solution)/shard_map/reshape | solution.py:261
  41.2 1.1 %reshape.16 = bf16[20,12,384]{2,1,0:T(8,128)(2,1)S(1)} reshape(bf16[20,2,2,3,24,16]{5,4,3,2,1,0:T(8,128)(2,1)S(1)} %copy.26) | data formatting | bytes 368640 | tf_op jit(solution)/shard_map/reshape | solution.py:261
  42.3 0.7 pad.4.qt
  43.0 32.7 %shard_map.100 = f32[4,16,128]{2,1,0:T(8,128)} custom-call(bf16[20,16,384]{2,1,0:T(8,128)(2,1)} %pad.4.qt, bf16[3,27,64]{2,1,0:T(8,128)(2,1)} %bitcast.17, bf16[3,768,27]{2,1,0:T(8,128)(2,1)} %constant.5.clone.sel, bf16[27,64,64]{2,1,0:T(8,128)(2,1)} %ew.1, bf16[8,64,128]{2,1,0:T(8,128)(2,1)} %bitcast.16, bf16[27,128,128]{2,1,0:T(8,128)(2,1)} %m1.1, ...), custom_call_target="tpu_custom_call" | custom-call | tf_op jit(solution)/shard_map/pallas_call | solution.py:218
  75.7 0.8 copy.23
  76.5 0.2 reshape.14
  76.8 1.3 %copy.24 = f32[3,4,16,2,8,2]{1,5,4,3,2,0:T(2,128)S(1)} copy(f32[3,4,16,2,8,2]{4,2,1,0,5,3:T(8,128)S(1)} %bitcast.14) | data formatting | bytes 49152 | tf_op jit(solution)/shard_map/transpose | solution.py:264
  78.1 0.4 copy.25
  78.5 0.7 convert_add_fusion
  (13 shorter events, 0.2 us)
Async XLA Ops:
  0.0 7.0 %collective-permute-start = (bf16[3,4,32,16]{2,3,1,0:T(8,128)(2,1)}, bf16[3,4,32,16]{2,3,1,0:T(8,128)(2,1)S(1)}, u32[]{:S(2)}, u32[]{:S(2)}) collective-permute-start(bf16[3,4,32,16]{2,3,1,0:T(8,128)(2,1)} %param.10), channel_id=1, source_target_pairs={{0,64},{32,96},{64,128},{96,160},{128,192},{160,224},{192,0},{224,... | collective-permute-start | bytes 36872 | tf_op jit(solution)/shard_map/ppermute | solution.py:249
  3.6 8.0 %collective-permute-start.2 = (bf16[3,4,32,16]{2,3,1,0:T(8,128)(2,1)}, bf16[3,4,32,16]{2,3,1,0:T(8,128)(2,1)S(1)}, u32[]{:S(2)}, u32[]{:S(2)}) collective-permute-start(bf16[3,4,32,16]{2,3,1,0:T(8,128)(2,1)} %param.10), channel_id=1, source_target_pairs={{0,224},{32,0},{64,32},{96,64},{128,96},{160,128},{192,160},{224,1... | collective-permute-start | bytes 36872 | tf_op jit(solution)/shard_map/ppermute | solution.py:249
  5.3 5.4 %collective-permute-start.1 = (bf16[3,4,32,16]{2,3,1,0:T(8,128)(2,1)}, bf16[3,4,32,16]{2,3,1,0:T(8,128)(2,1)S(1)}, u32[]{:S(2)}, u32[]{:S(2)}) collective-permute-start(bf16[3,4,32,16]{2,3,1,0:T(8,128)(2,1)} %param.10), channel_id=1, source_target_pairs={{0,32},{32,64},{64,96},{96,128},{128,160},{160,192},{192,224},{224... | collective-permute-start | bytes 36872 | tf_op jit(solution)/shard_map/ppermute | solution.py:249
  5.3 6.3 %collective-permute-start.3 = (bf16[3,4,32,16]{2,3,1,0:T(8,128)(2,1)}, bf16[3,4,32,16]{2,3,1,0:T(8,128)(2,1)S(1)}, u32[]{:S(2)}, u32[]{:S(2)}) collective-permute-start(bf16[3,4,32,16]{2,3,1,0:T(8,128)(2,1)} %param.10), channel_id=1, source_target_pairs={{0,192},{32,224},{64,0},{96,32},{128,64},{160,96},{192,128},{224,1... | collective-permute-start | bytes 36872 | tf_op jit(solution)/shard_map/ppermute | solution.py:249
  11.8 11.0 %collective-permute-start.4 = (bf16[3,20,8,16]{2,3,1,0:T(8,128)(2,1)S(1)}, bf16[3,20,8,16]{2,3,1,0:T(8,128)(2,1)S(1)}, u32[]{:S(2)}, u32[]{:S(2)}) collective-permute-start(bf16[3,20,8,16]{2,3,1,0:T(8,128)(2,1)S(1)} %get-tuple-element.7), channel_id=1, source_target_pairs={{0,8},{8,16},{16,24},{24,0},{1,9},{9,17},{17,25},{25,1},{2,10},{10... | collective-permute-start | bytes 46088 | tf_op jit(solution)/shard_map/ppermute | solution.py:249
  14.8 15.2 %collective-permute-start.5 = (bf16[3,20,8,16]{2,3,1,0:T(8,128)(2,1)S(1)}, bf16[3,20,8,16]{2,3,1,0:T(8,128)(2,1)S(1)}, u32[]{:S(2)}, u32[]{:S(2)}) collective-permute-start(bf16[3,20,8,16]{2,3,1,0:T(8,128)(2,1)S(1)} %get-tuple-element.8), channel_id=1, source_target_pairs={{0,24},{8,0},{16,8},{24,16},{1,25},{9,1},{17,9},{25,17},{2,26},{10... | collective-permute-start | bytes 46088 | tf_op jit(solution)/shard_map/ppermute | solution.py:249
  30.4 4.0 %collective-permute-start.6 = (bf16[3,20,48,8]{2,3,1,0:T(8,128)(2,1)S(1)}, bf16[3,20,48,8]{2,3,1,0:T(8,128)(2,1)S(1)}, u32[]{:S(2)}, u32[]{:S(2)}) collective-permute-start(bf16[3,20,48,8]{2,3,1,0:T(8,128)(2,1)S(1)} %get-tuple-element.5), channel_id=1, source_target_pairs={{0,1},{1,2},{2,3},{3,4},{4,5},{5,6},{6,7},{7,0},{8,9},{9,10},{10,1... | collective-permute-start | bytes 138248 | tf_op jit(solution)/shard_map/ppermute | solution.py:249
  32.5 4.3 %collective-permute-start.7 = (bf16[3,20,48,8]{2,3,1,0:T(8,128)(2,1)S(1)}, bf16[3,20,48,8]{2,3,1,0:T(8,128)(2,1)S(1)}, u32[]{:S(2)}, u32[]{:S(2)}) collective-permute-start(bf16[3,20,48,8]{2,3,1,0:T(8,128)(2,1)S(1)} %get-tuple-element.6), channel_id=1, source_target_pairs={{0,7},{1,0},{2,1},{3,2},{4,3},{5,4},{6,5},{7,6},{8,15},{9,8},{10,9... | collective-permute-start | bytes 138248 | tf_op jit(solution)/shard_map/ppermute | solution.py:249
  75.7 2.7 %copy-start = (bf16[3,4,32,16]{2,3,1,0:T(8,128)(2,1)S(1)}, bf16[3,4,32,16]{2,3,1,0:T(8,128)(2,1)}, u32[]{:S(2)}) copy-start(bf16[3,4,32,16]{2,3,1,0:T(8,128)(2,1)} %param.10) | copy-start | bytes 36868
where the time goes:
time: 79.3 us; the launch traced here: 79.1 us
  Pallas kernels  32.7 us (41%)
  waiting for transfers between devices  20.2 us (25%)
  starting transfers between devices  15.3 us (19%)
  local copies, waits for them, and re-layouts  9.66 us (12%)
  other arithmetic  1.17 us (1%)
    pallas_call x1, Pallas kernels, network(): pl.pallas_call(unet, out_shape=jax.ShapeDtypeStruct((4, 16, 128), F32), i...  32.7 us
    ppermute x8, waiting for transfers between devices, ring(): return lax.ppermute(value, axis, [(i, (i + step) % n) for i in range(n)])  20.2 us
    ppermute x8, starting transfers between devices, ring(): return lax.ppermute(value, axis, [(i, (i + step) % n) for i in range(n)])  15.3 us
    reshape x2, local copies, waits for them, and re-layouts, local(): wide.reshape(3, 20, 24, 2, 16, 2).transpose(1, 3, 5, 0, 2, 4)  3.85 us
  transfers between devices with their start and end apart: 8, of which 5 were waited for; matrix products, arithmetic and copies ran while one was open for 1% of the time, Pallas kernels for 0%

commit v1 on v0

--- a/solution.py
+++ b/solution.py
@@ -31,16 +31,106 @@
     return sel.reshape(3, 768, 27)
 
 
+def place_columns():
+    place = np.zeros((32, 256), np.float32)
+    for jy in range(2):
+        for lane in range(128):
+            place[2 * (lane // 8) + jy, 128 * jy + lane] = 1
+    return place
+
+
+def gather_rows():
+    rows = np.zeros((2, 64, 192), np.float32)
+    for jy in range(2):
+        for x in range(4):
+            for z in range(16):
+                for c in range(3):
+                    rows[jy, 16 * x + jy * 6 + (z % 2) * 3 + c, 64 * c + 16 * x + z] = 1
+    return rows
+
+
+def widen_lanes():
+    wide = np.zeros((384, 256), np.float32)
+    slab = np.zeros((384, 256), np.float32)
+    for piece, (first, shift) in enumerate(((0, 4), (4, -4), (0, 12))):
+        for z in range(first, 8 if piece < 2 else 4):
+            for y in range(16):
+                wide[128 * piece + 8 * y + z, 16 * y + z + shift] = 1
+            for i in range(4):
+                for y in range(4):
+                    slab[128 * piece + 32 * i + 8 * y + z, 64 * i + 16 * y + z + shift] = 1
+    return wide, slab
+
+
 def dot(a, b):
     return jnp.dot(a, b, preferred_element_type=F32)
 
 
+def remote(src, dst, send, recv, **where):
+    return pltpu.make_async_remote_copy(
+        src_ref=src, dst_ref=dst, send_sem=send, recv_sem=recv,
+        device_id=where, device_id_type=pl.DeviceIdType.MESH,
+    )
+
+
 def unet(
-    qt, lw, sel, ew, dw, m1, m2, uw, cw, hw,
+    disp, place, rows, lw_hbm, sel_hbm, wide_hbm, slab_hbm,
+    ew_hbm, dw_hbm, m1_hbm, m2_hbm, uw_hbm, cw_hbm, hw,
     out,
+    layers, left, right, slab_out, slab_in, sides, slabs, heads, qt,
+    lw, sel, wide, slab, ew, dw, m1, m2, uw, cw,
     patch, wl, we, wd, wm1, wm2, wu, wc, wh,
-    f0, f1, skip, coarse, middle, deep, ks, ku, joined,
+    f0, f1, skip, coarse, middle, deep, ks, ku,
+    load_sem, x_send, x_recv, n_send, n_recv,
 ):
+    gx, gy, gz = lax.axis_index("gx"), lax.axis_index("gy"), lax.axis_index("gz")
+    nx, ny, nz = lax.axis_size("gx"), lax.axis_size("gy"), lax.axis_size("gz")
+
+    def at_x(step):
+        return lax.rem(gx + nx + step, nx)
+
+    def at_yz(sy, sz):
+        return {"gy": lax.rem(gy + ny + sy, ny), "gz": lax.rem(gz + nz + sz, nz)}
+
+    around = [(sy, sz) for sy in (-1, 0, 1) for sz in (-1, 0, 1) if (sy, sz) != (0, 0)]
+    steps = (-2, -1, 1, 2)
+
+    barrier = pltpu.get_barrier_semaphore()
+    for step in steps:
+        pl.semaphore_signal(barrier, inc=1, device_id={"gx": at_x(step)}, device_id_type=pl.DeviceIdType.MESH)
+    for sy, sz in around:
+        pl.semaphore_signal(barrier, inc=1, device_id=at_yz(sy, sz), device_id_type=pl.DeviceIdType.MESH)
+
+    loads = [
+        pltpu.make_async_copy(src, dst, load_sem.at[n])
+        for n, (src, dst) in enumerate((
+            (lw_hbm, lw), (sel_hbm, sel), (ew_hbm, ew), (cw_hbm, cw), (m1_hbm, m1), (m2_hbm, m2),
+            (uw_hbm, uw), (dw_hbm, dw), (wide_hbm, wide), (slab_hbm, slab),
+        ))
+    ]
+    for load in loads:
+        load.start()
+
+    row_z = lax.broadcasted_iota(jnp.int32, (192, 128), 0) % 16 // 2
+    lane_z = lax.broadcasted_iota(jnp.int32, (192, 128), 1) % 8
+    keep = row_z == lane_z
+    cells = dot(disp[...].reshape(192, 32), place[...])
+    own = jnp.zeros((64, 128), F32)
+    for jy in range(2):
+        part = jnp.where(keep, cells[:, 128 * jy : 128 * jy + 128], 0.0).astype(BF)
+        own = own + dot(rows[jy], part)
+    layers[8:12] = own.astype(BF).reshape(4, 16, 128)
+
+    pl.semaphore_wait(barrier, 12)
+    x_copies = []
+    for n, step in enumerate(steps):
+        x_copies.append(remote(
+            layers.at[8:12], layers.at[pl.ds(8 - 4 * step, 4)], x_send.at[n], x_recv.at[n], gx=at_x(step)
+        ))
+        x_copies[-1].start()
+
+    for n in (0, 1, 2, 3):
+        loads[n].wait()
     w = dot(sel[0], lw[0]) + dot(sel[1], lw[1]) + dot(sel[2], lw[2])
     w = w.reshape(4, 192, 64)
     wl[:, 0:128] = jnp.concatenate([w[0], w[1]], axis=1).astype(BF)
@@ -56,8 +146,6 @@
 
     we[...] = jnp.zeros_like(we)
     wc[...] = jnp.zeros_like(wc)
-    wm1[...] = jnp.zeros_like(wm1)
-    wm2[...] = jnp.zeros_like(wm2)
     for a in range(3):
         for b in range(3):
             for m, tile in pair_tiles(ew, a, b):
@@ -77,6 +165,34 @@
                             for s in range(2):
                                 row = (((s * 3 + a) * 2 + dy) * 2 + dz) * 256 + (jy * 2 + jz) * 64
                                 wc[row : row + 64, oy * 128 : oy * 128 + 128] = tile[s * 64 : s * 64 + 64]
+
+    for copy in x_copies:
+        copy.wait_recv()
+    quarter = lax.broadcasted_iota(jnp.int32, (16, 128), 1) // 32
+    for g in range(5):
+        for side in range(2):
+            tile = jnp.zeros((16, 128), F32)
+            for i in range(4):
+                shift = (32 * i + 32 * (1 - side)) % 128
+                t = layers[4 * g + i].astype(F32)
+                tile = jnp.where(quarter == i, pltpu.roll(t, shift, axis=1) if shift else t, tile)
+            slab_out[side, g] = tile.astype(BF)
+    n_copies = []
+    for n, (sy, sz) in enumerate(around):
+        if sy == 0:
+            src, dst = layers, left if sz == 1 else right
+        else:
+            side = 0 if sy == 1 else 1
+            src, dst = slab_out.at[side], slab_in.at[side, (0, 1, 2)[sz]]
+        n_copies.append(remote(src, dst, n_send.at[n], n_recv.at[n], **at_yz(sy, sz)))
+        n_copies[-1].start()
+
+    for n in range(4, 10):
+        loads[n].wait()
+    wm1[...] = jnp.zeros_like(wm1)
+    wm2[...] = jnp.zeros_like(wm2)
+    for a in range(3):
+        for b in range(3):
             for c in range(3):
                 for src, dst in ((m1, wm1), (m2, wm2)):
                     tile = jnp.transpose(src[9 * a + 3 * b + c].astype(F32)).astype(BF)
@@ -95,9 +211,31 @@
     for g in range(4):
         wh[3 * g : 3 * g + 3, 64 * g : 64 * g + 64] = hw[...].astype(F32)
 
+    for copy in n_copies:
+        copy.wait_recv()
+    for n, src in enumerate((layers, left, right)):
+        sides[:, 128 * n : 128 * n + 128] = src[...].reshape(320, 128)
+        for side in range(2):
+            slabs[side, :, 128 * n : 128 * n + 128] = slab_in[side, n].reshape(80, 128)
+    mid = dot(sides[...], wide[...]).reshape(20, 16, 256)
+    half = lax.broadcasted_iota(jnp.int32, (20, 16, 128), 2) < 64
+    first, second = pltpu.roll(mid[:, :, :128], 64, axis=2), pltpu.roll(mid[:, :, 128:], 64, axis=2)
+    ends = [dot(slabs[side], slab[...]).reshape(5, 16, 256) for side in range(2)]
+    lows, highs = [], []
+    for i in range(4):
+        lane = 128 * (i // 2)
+        low, high = ends[0][:, :, lane : lane + 128], ends[1][:, :, lane : lane + 128]
+        lows.append(pltpu.roll(low, 64, axis=2) if i % 2 == 1 else low)
+        highs.append(pltpu.roll(high, 64, axis=2) if i % 2 == 0 else high)
+    low = jnp.stack(lows, axis=1).reshape(20, 16, 128)
+    high = jnp.stack(highs, axis=1).reshape(20, 16, 128)
+    qt[:, :, 0:128] = jnp.where(half, low, first)
+    qt[:, :, 128:256] = jnp.where(half, first, second)
+    qt[:, :, 256:384] = jnp.where(half, second, high)
+
     @pl.loop(0, 20)
     def _(x):
-        q = qt[x].astype(F32)
+        q = qt[x]
         for dy in range(2):
             for dz in range(2):
                 s = dy * 16 + dz
@@ -207,20 +345,53 @@
         v = act(dot(jnp.concatenate(taps, axis=1), wc[...])).astype(BF)
         for h in range(2):
             j = v[h * 128 : h * 128 + 128]
-            out[x + h] = lax.dot_general(
+            heads[x + h] = lax.dot_general(
                 wh[...].astype(BF), j, (((1,), (1,)), ((), ())), preferred_element_type=F32
             )
 
-
-def network(qt, lw, ew, dw, m1, m2, uw, cw, hw):
-    sel = jnp.asarray(lift_selection(), BF)
-    vm = pl.BlockSpec(memory_space=pltpu.VMEM)
-    return pl.pallas_call(
+    h = heads[...].reshape(64, 128)
+    coarse_part = h.astype(BF)
+    total = disp[...].astype(F32).reshape(192, 32)
+    for part in (coarse_part, (h - coarse_part.astype(F32)).astype(BF)):
+        for jy in range(2):
+            t = lax.dot_general(rows[jy], part, (((0,), (0,)), ((), ())), preferred_element_type=F32)
+            t = jnp.where(keep, t, 0.0).astype(BF)
+            total = total + lax.dot_general(
+                t, place[:, 128 * jy : 128 * jy + 128], (((1,), (1,)), ((), ())), preferred_element_type=F32
+            )
+    out[...] = total.reshape(3, 4, 16, 32)
+    for copy in x_copies + n_copies:
+        copy.wait_send()
+
+
+def local(d, lw, ew, dw, m1, m2, uw, cw, hw):
+    wide, slab = widen_lanes()
+    vm, anywhere = pl.BlockSpec(memory_space=pltpu.VMEM), pl.BlockSpec(memory_space=pl.ANY)
+    out = pl.pallas_call(
         unet,
-        out_shape=jax.ShapeDtypeStruct((4, 16, 128), F32),
-        in_specs=[vm] * 10,
+        out_shape=jax.ShapeDtypeStruct((3, 4, 16, 32), F32),
+        in_specs=[vm] * 3 + [anywhere] * 10 + [vm],
         out_specs=vm,
         scratch_shapes=[
+            pltpu.VMEM((20, 16, 128), BF),
+            pltpu.VMEM((20, 16, 128), BF),
+            pltpu.VMEM((20, 16, 128), BF),
+            pltpu.VMEM((2, 5, 16, 128), BF),
+            pltpu.VMEM((2, 3, 5, 16, 128), BF),
+            pltpu.VMEM((320, 384), BF),
+            pltpu.VMEM((2, 80, 384), BF),
+            pltpu.VMEM((4, 16, 128), F32),
+            pltpu.VMEM((20, 16, 384), F32),
+            pltpu.VMEM((3, 27, 64), BF),
+            pltpu.VMEM((3, 768, 27), BF),
+            pltpu.VMEM((384, 256), BF),
+            pltpu.VMEM((384, 256), BF),
+            pltpu.VMEM((27, 64, 64), BF),
+            pltpu.VMEM((8, 64, 128), BF),
+            pltpu.VMEM((27, 128, 128), BF),
+            pltpu.VMEM((27, 128, 128), BF),
+            pltpu.VMEM((8, 64, 128), BF),
+            pltpu.VMEM((27, 64, 128), BF),
             pltpu.VMEM((20, 64, 384), BF),
             pltpu.VMEM((192, 256), BF),
             pltpu.VMEM((3072, 256), BF),
@@ -238,31 +409,22 @@
             pltpu.VMEM((4, 144, 256), BF),
             pltpu.VMEM((2, 2, 6, 128, 256), BF),
             pltpu.VMEM((2, 2, 6, 128, 256), BF),
-            pltpu.VMEM((8, 128), F32),
+            pltpu.SemaphoreType.DMA((10,)),
+            pltpu.SemaphoreType.DMA((4,)),
+            pltpu.SemaphoreType.DMA((4,)),
+            pltpu.SemaphoreType.DMA((8,)),
+            pltpu.SemaphoreType.DMA((8,)),
         ],
-        compiler_params=pltpu.CompilerParams(vmem_limit_bytes=56 * 1024 * 1024),
-    )(qt, jnp.transpose(lw, (2, 0, 1)), sel, ew, jnp.transpose(dw, (0, 2, 1)), m1, m2, uw, cw, hw)
-
-
-def ring(value, axis, step):
-    n = lax.axis_size(axis)
-    return lax.ppermute(value, axis, [(i, (i + step) % n) for i in range(n)])
-
-
-def local(d, lw, ew, dw, m1, m2, uw, cw, hw):
-    wide = jnp.concatenate(
-        [ring(d, "gx", 2), ring(d, "gx", 1), d, ring(d, "gx", -1), ring(d, "gx", -2)], axis=1
+        compiler_params=pltpu.CompilerParams(
+            vmem_limit_bytes=58 * 1024 * 1024, collective_id=0, has_side_effects=True
+        ),
+    )(
+        jnp.transpose(d, (0, 1, 3, 2)), jnp.asarray(place_columns(), BF), jnp.asarray(gather_rows(), BF),
+        jnp.transpose(lw, (2, 0, 1)), jnp.asarray(lift_selection(), BF),
+        jnp.asarray(wide, BF), jnp.asarray(slab, BF),
+        ew, jnp.transpose(dw, (0, 2, 1)), m1, m2, uw, cw, hw,
     )
-    for axis, dim in (("gy", 2), ("gz", 3)):
-        size = wide.shape[dim]
-        head = lax.slice_in_dim(wide, 0, 8, axis=dim)
-        tail = lax.slice_in_dim(wide, size - 8, size, axis=dim)
-        wide = jnp.concatenate([ring(tail, axis, 1), wide, ring(head, axis, -1)], axis=dim)
-    qt = wide.reshape(3, 20, 24, 2, 16, 2).transpose(1, 3, 5, 0, 2, 4).reshape(20, 12, 384)
-    qt = jnp.pad(qt, ((0, 0), (0, 4), (0, 0)))
-    head = network(qt, lw, ew, dw, m1, m2, uw, cw, hw)
-    head = head[:, :12].reshape(4, 2, 2, 3, 16, 8).transpose(3, 0, 4, 1, 5, 2).reshape(3, 4, 32, 16)
-    return d.astype(F32) + head
+    return jnp.transpose(out, (0, 1, 3, 2))
 
 
 def solution(mesh):

time: 79.3 us -> 51.2 us (0.65)
  waiting for transfers between devices: 20.2 us -> 0 us
  Pallas kernels: 32.7 us -> 49.5 us
  starting transfers between devices: 15.3 us -> 0 us
  local copies, waits for them, and re-layouts: 9.66 us -> 1.54 us
  other arithmetic: 1.17 us -> 0 us
    ppermute x8 -> x0, waiting for transfers between devices: 20.2 us -> none  [ring(): return lax.ppermute(value, axis, [(i, (i + step) % n) for i in range(n)])]
    pallas_call x1, Pallas kernels: 32.7 us -> 49.5 us  [local(): pl.pallas_call(unet, out_shape=jax.ShapeDtypeStruct((3, 4, 16, 32), F32),...]
    ppermute x8 -> x0, starting transfers between devices: 15.3 us -> none  [ring(): return lax.ppermute(value, axis, [(i, (i + step) % n) for i in range(n)])]
    reshape x4 -> x0, local copies, waits for them, and re-layouts: 4.49 us -> none  [the longest x2 3.85 us: local(): wide.reshape(3, 20, 24, 2, 16, 2).transpose(1, 3, 5, 0, 2, 4)]
    concatenate x2 -> x0, local copies, waits for them, and re-layouts: 1.34 us -> none  [the longest x1 1.33 us: local(): jnp.concatenate([ring(tail, axis, 1), wide, ring(head, axis, -1)], axis=dim)]
    transpose x1 -> x0, local copies, waits for them, and re-layouts: 1.31 us -> none  [local(): head[:, :12].reshape(4, 2, 2, 3, 16, 8).transpose(3, 0, 4, 1, 5, 2)]
    slice x3 -> x0, local copies, waits for them, and re-layouts: 0.95 us -> none  [the longest x1 0.78 us: local(): head[:, :12].reshape(4, 2, 2, 3, 16, 8).transpose(3, 0, 4, 1, 5, 2)]
  transfers between devices with their start and end apart: 8 -> 0, of which waited for: 5 -> 0; matrix products, arithmetic and copies ran while one was open for 1% -> 0% of each run, Pallas kernels for 0% -> 0%
where the time goes in v1:
time: 51.2 us; the launch traced here: 51.1 us
  Pallas kernels  49.5 us (97%)
  local copies, waits for them, and re-layouts  1.54 us (3%)
    pallas_call x1, Pallas kernels, local(): pl.pallas_call(unet, out_shape=jax.ShapeDtypeStruct((3, 4, 16, 32), F32),...  49.5 us
    unnamed x1, local copies, waits for them, and re-layouts  1.54 us

profile of v1, /device:TPU:1, one launch (start us, length us, event | category | flops | bytes accessed | tf_op | source)
XLA Modules:
  0.0 51.1 jit_solution(16822223444822873229)
XLA Ops:
  0.0 49.5 %shard_map.136 = f32[3,4,16,32]{3,2,1,0:T(8,128)} custom-call(bf16[3,4,16,32]{3,2,1,0:T(8,128)(2,1)} %bitcast.6, bf16[32,256]{1,0:T(8,128)(2,1)} %constant.8.clone.place, bf16[2,64,192]{2,1,0:T(8,128)(2,1)} %constant.9.clone.rows, bf16[3,27,64]{2,1,0:T(8,128)(2,1)} %bitcast.7, bf16[3,768,27]{2,1,0:T(8,128)(2,1)} %constant.10.clone.sel_hbm, ...), custom_call_target="tpu_custom_call" | custom-call | tf_op jit(solution)/shard_map/pallas_call | solution.py:370
  49.5 1.5 %copy.16 = f32[3,4,32,16]{2,3,1,0:T(8,128)} copy(f32[3,4,32,16]{2,3,1,0:T(8,128)} %bitcast.4) | data formatting | bytes 49152

commit v2 on v1

--- a/solution.py
+++ b/solution.py
@@ -233,8 +233,7 @@
     qt[:, :, 128:256] = jnp.where(half, first, second)
     qt[:, :, 256:384] = jnp.where(half, second, high)
 
-    @pl.loop(0, 20)
-    def _(x):
+    def lay_patch(x):
         q = qt[x]
         for dy in range(2):
             for dz in range(2):
@@ -243,28 +242,23 @@
                 g = dy * 2 + dz
                 patch[x, 16 * g : 16 * g + 16, :] = r.astype(BF)
 
-    @pl.loop(0, 18)
-    def _(x):
-        p = patch[pl.ds(x, 3)].reshape(192, 384)
+    def lift(x):
+        p = patch[x : x + 3].reshape(192, 384)
         v = lax.dot_general(p, wl[...], (((0,), (0,)), ((), ())), preferred_element_type=F32)
         v = act(v)
         f0[x] = v.astype(BF)
         f1[x] = pltpu.roll(v, 383, axis=0).astype(BF)
 
-    @pl.loop(0, 8)
-    def _(i):
-        for h in range(2):
-            x = 2 * i + h
-            taps = []
-            for a in range(3):
-                for dy in range(2):
-                    for src in (f0, f1):
-                        taps.append(src[x + a, dy * 16 : dy * 16 + 352, :])
-            v = dot(jnp.concatenate(taps, axis=1), we[...])
-            skip[x] = act(v).astype(BF)
-
-    @pl.loop(0, 8)
-    def _(x):
+    def encode(x):
+        taps = []
+        for a in range(3):
+            for dy in range(2):
+                for src in (f0, f1):
+                    taps.append(src[x + a, dy * 16 : dy * 16 + 352, :])
+        v = dot(jnp.concatenate(taps, axis=1), we[...])
+        skip[x] = act(v).astype(BF)
+
+    def downward(x):
         lhs = jnp.concatenate([skip[2 * x], skip[2 * x + 1]], axis=1)
         v = act(dot(lhs, wd[...].reshape(512, 128)))
         for c in range(3):
@@ -273,31 +267,22 @@
             coarse[c, x, :, 0:128] = r[:, 0].reshape(176, 128).astype(BF)
             coarse[c, x, :, 128:256] = r[:, 1].reshape(176, 128).astype(BF)
 
-    @pl.loop(0, 3)
-    def _(i):
-        for h in range(2):
-            x = 2 * i + h
-            taps = []
-            for a in range(3):
-                for dy in range(2):
-                    for c in range(3):
-                        taps.append(coarse[c, x + a, dy * 16 : dy * 16 + 160, :])
-            v = act(dot(jnp.concatenate(taps, axis=1), wm1[...]))
-            for c in range(3):
-                r = pltpu.roll(v, 160 - c, axis=0) if c else v
-                middle[c, x] = r.astype(BF)
-
-    @pl.loop(0, 2)
-    def _(i):
-        for h in range(2):
-            x = 2 * i + h
-            taps = []
-            for a in range(3):
-                for dy in range(2):
-                    for c in range(3):
-                        taps.append(middle[c, x + a, dy * 16 : dy * 16 + 144, :])
-            v = act(dot(jnp.concatenate(taps, axis=1), wm2[...]))
-            deep[x] = v.astype(BF)
+    def conv_half(src, x, size, weight):
+        taps = []
+        for a in range(3):
+            for dy in range(2):
+                for c in range(3):
+                    taps.append(src[c, x + a, dy * 16 : dy * 16 + size, :])
+        return act(dot(jnp.concatenate(taps, axis=1), weight[...]))
+
+    def conv_first(x):
+        v = conv_half(coarse, x, 160, wm1)
+        for c in range(3):
+            r = pltpu.roll(v, 160 - c, axis=0) if c else v
+            middle[c, x] = r.astype(BF)
+
+    def conv_second(x):
+        deep[x] = conv_half(middle, x, 144, wm2).astype(BF)
 
     low = lax.broadcasted_iota(jnp.int32, (17, 16, 128), 2) < 64
 
@@ -308,8 +293,7 @@
             for dy in range(2):
                 dst[dy, dz, f] = r[dy : dy + 16].reshape(128, 256).astype(BF)
 
-    @pl.loop(0, 6)
-    def _(f):
+    def spread_skip(f):
         v = skip[f + 5].astype(F32).reshape(22, 16, 256)
         halves = []
         for jy in range(2):
@@ -318,8 +302,7 @@
             halves.append(pltpu.roll(t, 64, axis=2))
         spread(ks, f, jnp.concatenate(halves, axis=2))
 
-    @pl.loop(0, 6)
-    def _(f):
+    def upsample(f):
         xd = (f + 1) // 2
         a = (f + 1) % 2
         d = deep[xd]
@@ -333,21 +316,43 @@
             halves.append(jnp.where(low, s, pltpu.roll(s, 15, axis=1)))
         spread(ku, f, jnp.concatenate(halves, axis=2))
 
-    @pl.loop(0, 2)
-    def _(i):
-        x = 2 * i
+    def decode(x, n):
         taps = []
         for src in (ks, ku):
             for a in range(3):
                 for dy in range(2):
                     for dz in range(2):
-                        taps.append(src[dy, dz, pl.ds(x + a, 2)].reshape(256, 256))
+                        taps.append(src[dy, dz, x + a : x + a + n].reshape(128 * n, 256))
         v = act(dot(jnp.concatenate(taps, axis=1), wc[...])).astype(BF)
-        for h in range(2):
-            j = v[h * 128 : h * 128 + 128]
+        for h in range(n):
             heads[x + h] = lax.dot_general(
-                wh[...].astype(BF), j, (((1,), (1,)), ((), ())), preferred_element_type=F32
+                wh[...].astype(BF), v[h * 128 : h * 128 + 128], (((1,), (1,)), ((), ())), preferred_element_type=F32
             )
+
+    for x in range(20):
+        lay_patch(x)
+    for x in range(3):
+        lift(x)
+    for x in range(16):
+        if x + 3 < 18:
+            lift(x + 3)
+        encode(x)
+        if x % 2 == 1 and x > 1:
+            downward(x // 2 - 1)
+    spread_skip(0)
+    downward(7)
+    for x in range(6):
+        conv_first(x)
+        if x:
+            spread_skip(x)
+    for x in range(4):
+        conv_second(x)
+        for f in range(6):
+            if (f + 1) // 2 == x - 1:
+                upsample(f)
+    upsample(5)
+    decode(0, 2)
+    decode(2, 2)
 
     h = heads[...].reshape(64, 128)
     coarse_part = h.astype(BF)

time: 51.2 us -> 42.2 us (0.82)
  Pallas kernels: 49.5 us -> 40.5 us
    pallas_call x1, Pallas kernels: 49.5 us -> 40.5 us  [local(): pl.pallas_call(unet, out_shape=jax.ShapeDtypeStruct((3, 4, 16, 32), F32),...]
where the time goes in v2:
time: 42.2 us; the launch traced here: 42 us
  Pallas kernels  40.5 us (96%)
  local copies, waits for them, and re-layouts  1.54 us (4%)
    pallas_call x1, Pallas kernels, local(): pl.pallas_call(unet, out_shape=jax.ShapeDtypeStruct((3, 4, 16, 32), F32),...  40.5 us
    unnamed x1, local copies, waits for them, and re-layouts  1.54 us

profile of v2, /device:TPU:1, one launch (start us, length us, event | category | flops | bytes accessed | tf_op | source)
XLA Modules:
  0.0 42.0 jit_solution(16940205179442336390)
XLA Ops:
  0.0 40.5 %shard_map.136 = f32[3,4,16,32]{3,2,1,0:T(8,128)} custom-call(bf16[3,4,16,32]{3,2,1,0:T(8,128)(2,1)} %bitcast.6, bf16[32,256]{1,0:T(8,128)(2,1)} %constant.8.clone.place, bf16[2,64,192]{2,1,0:T(8,128)(2,1)} %constant.9.clone.rows, bf16[3,27,64]{2,1,0:T(8,128)(2,1)} %bitcast.7, bf16[3,768,27]{2,1,0:T(8,128)(2,1)} %constant.10.clone.sel_hbm, ...), custom_call_target="tpu_custom_call" | custom-call | tf_op jit(solution)/shard_map/pallas_call | solution.py:375
  40.5 1.5 %copy.16 = f32[3,4,32,16]{2,3,1,0:T(8,128)} copy(f32[3,4,32,16]{2,3,1,0:T(8,128)} %bitcast.4) | data formatting | bytes 49152

commit v3 on v2

--- a/solution.py
+++ b/solution.py
@@ -51,15 +51,11 @@
 
 def widen_lanes():
     wide = np.zeros((384, 256), np.float32)
-    slab = np.zeros((384, 256), np.float32)
-    for piece, (first, shift) in enumerate(((0, 4), (4, -4), (0, 12))):
-        for z in range(first, 8 if piece < 2 else 4):
+    for piece, (first, last, shift) in enumerate(((0, 8, 4), (4, 8, -4), (0, 4, 12))):
+        for z in range(first, last):
             for y in range(16):
                 wide[128 * piece + 8 * y + z, 16 * y + z + shift] = 1
-            for i in range(4):
-                for y in range(4):
-                    slab[128 * piece + 32 * i + 8 * y + z, 64 * i + 16 * y + z + shift] = 1
-    return wide, slab
+    return wide
 
 
 def dot(a, b):
@@ -74,42 +70,44 @@
 
 
 def unet(
-    disp, place, rows, lw_hbm, sel_hbm, wide_hbm, slab_hbm,
-    ew_hbm, dw_hbm, m1_hbm, m2_hbm, uw_hbm, cw_hbm, hw,
+    disp_hbm, place_hbm, rows_hbm, lw_hbm, sel_hbm, ew_hbm, cw_hbm, wide_hbm,
+    m1_hbm, m2_hbm, uw_hbm, dw_hbm, hw_hbm,
     out,
-    layers, left, right, slab_out, slab_in, sides, slabs, heads, qt,
-    lw, sel, wide, slab, ew, dw, m1, m2, uw, cw,
-    patch, wl, we, wd, wm1, wm2, wu, wc, wh,
+    disp, place, rows, lw, sel, ew, cw, wide, m1, m2, uw, dw, hw,
+    layers, left, right, slab_out, slab_in, sides, heads, mid,
+    patch, edge, wl, we, wd, wm1, wm2, wu, wc, wh,
     f0, f1, skip, coarse, middle, deep, ks, ku,
-    load_sem, x_send, x_recv, n_send, n_recv,
+    load_sem, x_send, x_recv, z_send, z_recv, y_send, y_recv,
 ):
     gx, gy, gz = lax.axis_index("gx"), lax.axis_index("gy"), lax.axis_index("gz")
     nx, ny, nz = lax.axis_size("gx"), lax.axis_size("gy"), lax.axis_size("gz")
 
     def at_x(step):
-        return lax.rem(gx + nx + step, nx)
-
-    def at_yz(sy, sz):
-        return {"gy": lax.rem(gy + ny + sy, ny), "gz": lax.rem(gz + nz + sz, nz)}
-
-    around = [(sy, sz) for sy in (-1, 0, 1) for sz in (-1, 0, 1) if (sy, sz) != (0, 0)]
+        return {"gx": lax.rem(gx + nx + step, nx)}
+
+    def at_y(step):
+        return {"gy": lax.rem(gy + ny + step, ny)}
+
+    def at_z(step):
+        return {"gz": lax.rem(gz + nz + step, nz)}
+
     steps = (-2, -1, 1, 2)
-
     barrier = pltpu.get_barrier_semaphore()
-    for step in steps:
-        pl.semaphore_signal(barrier, inc=1, device_id={"gx": at_x(step)}, device_id_type=pl.DeviceIdType.MESH)
-    for sy, sz in around:
-        pl.semaphore_signal(barrier, inc=1, device_id=at_yz(sy, sz), device_id_type=pl.DeviceIdType.MESH)
+    for where in [at_x(step) for step in steps] + [at_y(-1), at_y(1), at_z(-1), at_z(1)]:
+        pl.semaphore_signal(barrier, inc=1, device_id=where, device_id_type=pl.DeviceIdType.MESH)
 
     loads = [
         pltpu.make_async_copy(src, dst, load_sem.at[n])
         for n, (src, dst) in enumerate((
-            (lw_hbm, lw), (sel_hbm, sel), (ew_hbm, ew), (cw_hbm, cw), (m1_hbm, m1), (m2_hbm, m2),
-            (uw_hbm, uw), (dw_hbm, dw), (wide_hbm, wide), (slab_hbm, slab),
+            (disp_hbm, disp), (place_hbm, place), (rows_hbm, rows),
+            (lw_hbm, lw), (sel_hbm, sel), (ew_hbm, ew), (cw_hbm, cw), (wide_hbm, wide),
+            (m1_hbm, m1), (m2_hbm, m2), (uw_hbm, uw), (dw_hbm, dw), (hw_hbm, hw),
         ))
     ]
     for load in loads:
         load.start()
+    for load in loads[:3]:
+        load.wait()
 
     row_z = lax.broadcasted_iota(jnp.int32, (192, 128), 0) % 16 // 2
     lane_z = lax.broadcasted_iota(jnp.int32, (192, 128), 1) % 8
@@ -121,16 +119,16 @@
         own = own + dot(rows[jy], part)
     layers[8:12] = own.astype(BF).reshape(4, 16, 128)
 
-    pl.semaphore_wait(barrier, 12)
+    pl.semaphore_wait(barrier, 8)
     x_copies = []
     for n, step in enumerate(steps):
         x_copies.append(remote(
-            layers.at[8:12], layers.at[pl.ds(8 - 4 * step, 4)], x_send.at[n], x_recv.at[n], gx=at_x(step)
+            layers.at[8:12], layers.at[pl.ds(8 - 4 * step, 4)], x_send.at[n], x_recv.at[n], **at_x(step)
         ))
         x_copies[-1].start()
 
-    for n in (0, 1, 2, 3):
-        loads[n].wait()
+    for load in loads[3:7]:
+        load.wait()
     w = dot(sel[0], lw[0]) + dot(sel[1], lw[1]) + dot(sel[2], lw[2])
     w = w.reshape(4, 192, 64)
     wl[:, 0:128] = jnp.concatenate([w[0], w[1]], axis=1).astype(BF)
@@ -168,27 +166,15 @@
 
     for copy in x_copies:
         copy.wait_recv()
-    quarter = lax.broadcasted_iota(jnp.int32, (16, 128), 1) // 32
-    for g in range(5):
-        for side in range(2):
-            tile = jnp.zeros((16, 128), F32)
-            for i in range(4):
-                shift = (32 * i + 32 * (1 - side)) % 128
-                t = layers[4 * g + i].astype(F32)
-                tile = jnp.where(quarter == i, pltpu.roll(t, shift, axis=1) if shift else t, tile)
-            slab_out[side, g] = tile.astype(BF)
-    n_copies = []
-    for n, (sy, sz) in enumerate(around):
-        if sy == 0:
-            src, dst = layers, left if sz == 1 else right
-        else:
-            side = 0 if sy == 1 else 1
-            src, dst = slab_out.at[side], slab_in.at[side, (0, 1, 2)[sz]]
-        n_copies.append(remote(src, dst, n_send.at[n], n_recv.at[n], **at_yz(sy, sz)))
-        n_copies[-1].start()
-
-    for n in range(4, 10):
-        loads[n].wait()
+    z_copies = [
+        remote(layers, left, z_send.at[0], z_recv.at[0], **at_z(1)),
+        remote(layers, right, z_send.at[1], z_recv.at[1], **at_z(-1)),
+    ]
+    for copy in z_copies:
+        copy.start()
+
+    for load in loads[7:]:
+        load.wait()
     wm1[...] = jnp.zeros_like(wm1)
     wm2[...] = jnp.zeros_like(wm2)
     for a in range(3):
@@ -211,52 +197,78 @@
     for g in range(4):
         wh[3 * g : 3 * g + 3, 64 * g : 64 * g + 64] = hw[...].astype(F32)
 
-    for copy in n_copies:
+    for copy in z_copies:
         copy.wait_recv()
     for n, src in enumerate((layers, left, right)):
         sides[:, 128 * n : 128 * n + 128] = src[...].reshape(320, 128)
-        for side in range(2):
-            slabs[side, :, 128 * n : 128 * n + 128] = slab_in[side, n].reshape(80, 128)
-    mid = dot(sides[...], wide[...]).reshape(20, 16, 256)
-    half = lax.broadcasted_iota(jnp.int32, (20, 16, 128), 2) < 64
-    first, second = pltpu.roll(mid[:, :, :128], 64, axis=2), pltpu.roll(mid[:, :, 128:], 64, axis=2)
-    ends = [dot(slabs[side], slab[...]).reshape(5, 16, 256) for side in range(2)]
-    lows, highs = [], []
-    for i in range(4):
-        lane = 128 * (i // 2)
-        low, high = ends[0][:, :, lane : lane + 128], ends[1][:, :, lane : lane + 128]
-        lows.append(pltpu.roll(low, 64, axis=2) if i % 2 == 1 else low)
-        highs.append(pltpu.roll(high, 64, axis=2) if i % 2 == 0 else high)
-    low = jnp.stack(lows, axis=1).reshape(20, 16, 128)
-    high = jnp.stack(highs, axis=1).reshape(20, 16, 128)
-    qt[:, :, 0:128] = jnp.where(half, low, first)
-    qt[:, :, 128:256] = jnp.where(half, first, second)
-    qt[:, :, 256:384] = jnp.where(half, second, high)
-
-    def lay_patch(x):
-        q = qt[x]
+    mid[...] = dot(sides[...], wide[...]).reshape(20, 16, 256)
+    half = lax.broadcasted_iota(jnp.int32, (10, 16, 128), 2) < 64
+    pairs = mid[...].reshape(10, 2, 16, 256)
+    upper = jnp.where(half, pltpu.roll(pairs[:, 0, :, 128:], 64, axis=2), pairs[:, 1, :, 128:])
+    lower = jnp.where(half, pairs[:, 0, :, :128], pltpu.roll(pairs[:, 1, :, :128], 64, axis=2))
+    slab_out[0] = upper.astype(BF)
+    slab_out[1] = lower.astype(BF)
+    y_copies = [
+        remote(slab_out.at[0], slab_in.at[0], y_send.at[0], y_recv.at[0], **at_y(1)),
+        remote(slab_out.at[1], slab_in.at[1], y_send.at[1], y_recv.at[1], **at_y(-1)),
+    ]
+    for copy in y_copies:
+        copy.start()
+
+    def lay_inner(x):
+        q = mid[x]
         for dy in range(2):
             for dz in range(2):
-                s = dy * 16 + dz
-                r = pltpu.roll(q, 384 - s, axis=1) if s else q
+                shift = dy * 16 + dz
+                r = pltpu.roll(q, 256 - shift, axis=1) if shift else q
                 g = dy * 2 + dz
                 patch[x, 16 * g : 16 * g + 16, :] = r.astype(BF)
 
-    def lift(x):
-        p = patch[x : x + 3].reshape(192, 384)
+    lane = lax.broadcasted_iota(jnp.int32, (16, 128), 1)
+
+    def lay_outer(x):
+        first, last = mid[x, :, 0:128], mid[x, :, 128:256]
+        low, high = slab_in[0, x // 2].astype(F32), slab_in[1, x // 2].astype(F32)
+        if x % 2:
+            low, high = pltpu.roll(low, 64, axis=1), pltpu.roll(high, 64, axis=1)
+        one = jnp.where(lane < 64, low, jnp.where(lane < 80, pltpu.roll(last, 80, axis=1), pltpu.roll(high, 80, axis=1)))
+        two = jnp.where(lane < 48, pltpu.roll(low, 112, axis=1), jnp.where(lane < 64, pltpu.roll(first, 48, axis=1), pltpu.roll(high, 64, axis=1)))
+        for dy, q in enumerate((one, two)):
+            for dz in range(2):
+                r = pltpu.roll(q, 127, axis=1) if dz else q
+                g = dy * 2 + dz
+                edge[x, 16 * g : 16 * g + 16, :] = r.astype(BF)
+
+    def lift(src, x, size):
+        p = src[x : x + 3].reshape(192, size)
         v = lax.dot_general(p, wl[...], (((0,), (0,)), ((), ())), preferred_element_type=F32)
-        v = act(v)
-        f0[x] = v.astype(BF)
-        f1[x] = pltpu.roll(v, 383, axis=0).astype(BF)
-
-    def encode(x):
+        return act(v)
+
+    def lift_inner(x):
+        v = lift(patch, x, 256)
+        f0[x, 64:304] = v[:240].astype(BF)
+        f1[x, 64:304] = pltpu.roll(v, 255, axis=0)[:240].astype(BF)
+
+    def lift_outer(x):
+        v = lift(edge, x, 128)
+        for dst, r in ((f0, v), (f1, pltpu.roll(v, 127, axis=0))):
+            dst[x, 0:64] = r[:64].astype(BF)
+            dst[x, 304:368] = r[64:].astype(BF)
+
+    def encode(x, n, spans):
         taps = []
         for a in range(3):
             for dy in range(2):
                 for src in (f0, f1):
-                    taps.append(src[x + a, dy * 16 : dy * 16 + 352, :])
-        v = dot(jnp.concatenate(taps, axis=1), we[...])
-        skip[x] = act(v).astype(BF)
+                    taps.append(jnp.concatenate(
+                        [src[x + a + h, r + dy * 16 : r + dy * 16 + size, :] for h in range(n) for r, size in spans], axis=0
+                    ))
+        v = act(dot(jnp.concatenate(taps, axis=1), we[...])).astype(BF)
+        at = 0
+        for h in range(n):
+            for r, size in spans:
+                skip[x + h, r : r + size] = v[at : at + size]
+                at += size
 
     def downward(x):
         lhs = jnp.concatenate([skip[2 * x], skip[2 * x + 1]], axis=1)
@@ -330,15 +342,29 @@
             )
 
     for x in range(20):
-        lay_patch(x)
-    for x in range(3):
-        lift(x)
-    for x in range(16):
-        if x + 3 < 18:
-            lift(x + 3)
-        encode(x)
-        if x % 2 == 1 and x > 1:
+        lay_inner(x)
+    for x in range(4):
+        lift_inner(x)
+    for x in range(0, 16, 2):
+        for h in range(2):
+            if x + 4 + h < 18:
+                lift_inner(x + 4 + h)
+        encode(x, 2, ((64, 224),))
+    for copy in y_copies:
+        copy.wait_recv()
+    for x in range(20):
+        lay_outer(x)
+    for x in range(6):
+        lift_outer(x)
+    for x in range(0, 16, 4):
+        for h in range(4):
+            if x + 6 + h < 18:
+                lift_outer(x + 6 + h)
+        encode(x, 4, ((0, 64), (288, 64)))
+        if x:
+            downward(x // 2 - 2)
             downward(x // 2 - 1)
+    downward(6)
     spread_skip(0)
     downward(7)
     for x in range(6):
@@ -356,7 +382,7 @@
 
     h = heads[...].reshape(64, 128)
     coarse_part = h.astype(BF)
-    total = disp[...].astype(F32).reshape(192, 32)
+    total = jnp.zeros((192, 32), F32)
     for part in (coarse_part, (h - coarse_part.astype(F32)).astype(BF)):
         for jy in range(2):
             t = lax.dot_general(rows[jy], part, (((0,), (0,)), ((), ())), preferred_element_type=F32)
@@ -365,39 +391,33 @@
                 t, place[:, 128 * jy : 128 * jy + 128], (((1,), (1,)), ((), ())), preferred_element_type=F32
             )
     out[...] = total.reshape(3, 4, 16, 32)
-    for copy in x_copies + n_copies:
+    for copy in x_copies + z_copies + y_copies:
         copy.wait_send()
 
 
 def local(d, lw, ew, dw, m1, m2, uw, cw, hw):
-    wide, slab = widen_lanes()
-    vm, anywhere = pl.BlockSpec(memory_space=pltpu.VMEM), pl.BlockSpec(memory_space=pl.ANY)
+    anywhere = pl.BlockSpec(memory_space=pl.ANY)
+    args = (
+        jnp.transpose(d, (0, 1, 3, 2)), jnp.asarray(place_columns(), BF), jnp.asarray(gather_rows(), BF),
+        jnp.transpose(lw, (2, 0, 1)), jnp.asarray(lift_selection(), BF), ew, cw, jnp.asarray(widen_lanes(), BF),
+        m1, m2, uw, jnp.transpose(dw, (0, 2, 1)), hw,
+    )
     out = pl.pallas_call(
         unet,
         out_shape=jax.ShapeDtypeStruct((3, 4, 16, 32), F32),
-        in_specs=[vm] * 3 + [anywhere] * 10 + [vm],
-        out_specs=vm,
-        scratch_shapes=[
+        in_specs=[anywhere] * 13,
+        out_specs=pl.BlockSpec(memory_space=pltpu.VMEM),
+        scratch_shapes=[pltpu.VMEM(arg.shape, arg.dtype) for arg in args] + [
             pltpu.VMEM((20, 16, 128), BF),
             pltpu.VMEM((20, 16, 128), BF),
             pltpu.VMEM((20, 16, 128), BF),
-            pltpu.VMEM((2, 5, 16, 128), BF),
-            pltpu.VMEM((2, 3, 5, 16, 128), BF),
+            pltpu.VMEM((2, 10, 16, 128), BF),
+            pltpu.VMEM((2, 10, 16, 128), BF),
             pltpu.VMEM((320, 384), BF),
-            pltpu.VMEM((2, 80, 384), BF),
             pltpu.VMEM((4, 16, 128), F32),
-            pltpu.VMEM((20, 16, 384), F32),
-            pltpu.VMEM((3, 27, 64), BF),
-            pltpu.VMEM((3, 768, 27), BF),
-            pltpu.VMEM((384, 256), BF),
-            pltpu.VMEM((384, 256), BF),
-            pltpu.VMEM((27, 64, 64), BF),
-            pltpu.VMEM((8, 64, 128), BF),
-            pltpu.VMEM((27, 128, 128), BF),
-            pltpu.VMEM((27, 128, 128), BF),
-            pltpu.VMEM((8, 64, 128), BF),
-            pltpu.VMEM((27, 64, 128), BF),
-            pltpu.VMEM((20, 64, 384), BF),
+            pltpu.VMEM((20, 16, 256), F32),
+            pltpu.VMEM((20, 64, 256), BF),
+            pltpu.VMEM((20, 64, 128), BF),
             pltpu.VMEM((192, 256), BF),
             pltpu.VMEM((3072, 256), BF),
             pltpu.VMEM((2, 256, 128), BF),
@@ -406,30 +426,27 @@
             pltpu.VMEM((2, 128, 256), BF),
             pltpu.VMEM((6144, 256), BF),
             pltpu.VMEM((16, 256), F32),
-            pltpu.VMEM((18, 384, 256), BF),
-            pltpu.VMEM((18, 384, 256), BF),
+            pltpu.VMEM((18, 368, 256), BF),
+            pltpu.VMEM((18, 368, 256), BF),
             pltpu.VMEM((16, 352, 256), BF),
             pltpu.VMEM((3, 8, 176, 256), BF),
             pltpu.VMEM((3, 6, 160, 256), BF),
             pltpu.VMEM((4, 144, 256), BF),
             pltpu.VMEM((2, 2, 6, 128, 256), BF),
             pltpu.VMEM((2, 2, 6, 128, 256), BF),
-            pltpu.SemaphoreType.DMA((10,)),
+            pltpu.SemaphoreType.DMA((13,)),
             pltpu.SemaphoreType.DMA((4,)),
             pltpu.SemaphoreType.DMA((4,)),
-            pltpu.SemaphoreType.DMA((8,)),
-            pltpu.SemaphoreType.DMA((8,)),
+            pltpu.SemaphoreType.DMA((2,)),
+            pltpu.SemaphoreType.DMA((2,)),
+            pltpu.SemaphoreType.DMA((2,)),
+            pltpu.SemaphoreType.DMA((2,)),
         ],
         compiler_params=pltpu.CompilerParams(
             vmem_limit_bytes=58 * 1024 * 1024, collective_id=0, has_side_effects=True
         ),
-    )(
-        jnp.transpose(d, (0, 1, 3, 2)), jnp.asarray(place_columns(), BF), jnp.asarray(gather_rows(), BF),
-        jnp.transpose(lw, (2, 0, 1)), jnp.asarray(lift_selection(), BF),
-        jnp.asarray(wide, BF), jnp.asarray(slab, BF),
-        ew, jnp.transpose(dw, (0, 2, 1)), m1, m2, uw, cw, hw,
-    )
-    return jnp.transpose(out, (0, 1, 3, 2))
+    )(*args)
+    return d.astype(F32) + jnp.transpose(out, (0, 1, 3, 2))
 
 
 def solution(mesh):

time: 42.2 us -> 39.5 us (0.936)
  Pallas kernels: 40.5 us -> 37.8 us
  other arithmetic: 0 us -> 1.54 us
  local copies, waits for them, and re-layouts: 1.54 us -> 0.01 us
    pallas_call x1, Pallas kernels: 40.5 us -> 37.8 us  [local(): pl.pallas_call(unet, out_shape=jax.ShapeDtypeStruct((3, 4, 16, 32), F32),...]
    add x0 -> x1, other arithmetic: none -> 1.54 us  [local(): return d.astype(F32) + jnp.transpose(out, (0, 1, 3, 2))]
    unnamed x1 -> x2, local copies, waits for them, and re-layouts: 1.54 us -> 0.01 us
where the time goes in v3:
time: 39.5 us; the launch traced here: 39.4 us
  Pallas kernels  37.8 us (96%)
  other arithmetic  1.54 us (4%)
    pallas_call x1, Pallas kernels, local(): pl.pallas_call(unet, out_shape=jax.ShapeDtypeStruct((3, 4, 16, 32), F32),...  37.8 us
    add x1, other arithmetic, local(): return d.astype(F32) + jnp.transpose(out, (0, 1, 3, 2))  1.54 us

profile of v3, /device:TPU:1, one launch (start us, length us, event | category | flops | bytes accessed | tf_op | source)
XLA Modules:
  0.0 39.4 jit_solution(5641625197095229480)
XLA Ops:
  0.0 0.0 copy-start
  0.0 37.8 %shard_map.127 = f32[3,4,16,32]{3,2,1,0:T(8,128)} custom-call(bf16[3,4,16,32]{3,2,1,0:T(8,128)(2,1)} %bitcast.5, bf16[32,256]{1,0:T(8,128)(2,1)} %constant.8.clone.place_hbm, bf16[2,64,192]{2,1,0:T(8,128)(2,1)} %constant.9.clone.rows_hbm, bf16[3,27,64]{2,1,0:T(8,128)(2,1)} %bitcast.7, bf16[3,768,27]{2,1,0:T(8,128)(2,1)} %constant.10.clone.sel_hbm, ...), custom_call_target="tpu_custom_call" | custom-call | tf_op jit(solution)/shard_map/pallas_call | solution.py:405
  37.8 0.0 copy-done
  37.8 1.5 %bitcast_add_fusion = f32[3,4,32,16]{2,3,1,0:T(8,128)} fusion(f32[3,4,16,32]{3,2,1,0:T(8,128)} %shard_map.127, bf16[3,4,32,16]{2,3,1,0:T(8,128)(2,1)S(1)} %copy-done), kind=kLoop, calls=%fused_computation | loop fusion | flops 12288 | bytes 61440 | tf_op jit(solution)/shard_map/add | solution.py:449
Async XLA Ops:
  0.0 37.8 %copy-start = (bf16[3,4,32,16]{2,3,1,0:T(8,128)(2,1)S(1)}, bf16[3,4,32,16]{2,3,1,0:T(8,128)(2,1)}, u32[]{:S(2)}) copy-start(bf16[3,4,32,16]{2,3,1,0:T(8,128)(2,1)} %param.13) | copy-start | bytes 36868

commit v4 on v3

--- a/solution.py
+++ b/solution.py
@@ -49,6 +49,15 @@
     return rows
 
 
+def spread_head():
+    spread = np.zeros((96, 16), np.float32)
+    for jy in range(2):
+        for k in range(3):
+            for z in range(16):
+                spread[48 * jy + 16 * k + z, jy * 6 + (z % 2) * 3 + k] = 1
+    return spread
+
+
 def widen_lanes():
     wide = np.zeros((384, 256), np.float32)
     for piece, (first, last, shift) in enumerate(((0, 8, 4), (4, 8, -4), (0, 4, 12))):
@@ -71,10 +80,10 @@
 
 def unet(
     disp_hbm, place_hbm, rows_hbm, lw_hbm, sel_hbm, ew_hbm, cw_hbm, wide_hbm,
-    m1_hbm, m2_hbm, uw_hbm, dw_hbm, hw_hbm,
+    m1_hbm, m2_hbm, uw_hbm, dw_hbm, hw_hbm, spr_hbm,
     out,
-    disp, place, rows, lw, sel, ew, cw, wide, m1, m2, uw, dw, hw,
-    layers, left, right, slab_out, slab_in, sides, heads, mid,
+    disp, place, rows, lw, sel, ew, cw, wide, m1, m2, uw, dw, hw, spr,
+    layers, left, right, slab_out, slab_in, sides, whs, mid,
     patch, edge, wl, we, wd, wm1, wm2, wu, wc, wh,
     f0, f1, skip, coarse, middle, deep, ks, ku,
     load_sem, x_send, x_recv, z_send, z_recv, y_send, y_recv,
@@ -101,7 +110,7 @@
         for n, (src, dst) in enumerate((
             (disp_hbm, disp), (place_hbm, place), (rows_hbm, rows),
             (lw_hbm, lw), (sel_hbm, sel), (ew_hbm, ew), (cw_hbm, cw), (wide_hbm, wide),
-            (m1_hbm, m1), (m2_hbm, m2), (uw_hbm, uw), (dw_hbm, dw), (hw_hbm, hw),
+            (m1_hbm, m1), (m2_hbm, m2), (uw_hbm, uw), (dw_hbm, dw), (hw_hbm, hw), (spr_hbm, spr),
         ))
     ]
     for load in loads:
@@ -196,6 +205,7 @@
     wh[...] = jnp.zeros_like(wh)
     for g in range(4):
         wh[3 * g : 3 * g + 3, 64 * g : 64 * g + 64] = hw[...].astype(F32)
+    whs[...] = dot(spr[...], wh[...].astype(BF)).astype(BF)
 
     for copy in z_copies:
         copy.wait_recv()
@@ -335,32 +345,35 @@
                 for dy in range(2):
                     for dz in range(2):
                         taps.append(src[dy, dz, x + a : x + a + n].reshape(128 * n, 256))
-        v = act(dot(jnp.concatenate(taps, axis=1), wc[...])).astype(BF)
-        for h in range(n):
-            heads[x + h] = lax.dot_general(
-                wh[...].astype(BF), v[h * 128 : h * 128 + 128], (((1,), (1,)), ((), ())), preferred_element_type=F32
-            )
-
-    for x in range(20):
+        return act(dot(jnp.concatenate(taps, axis=1), wc[...])).astype(BF)
+
+    for x in range(6):
         lay_inner(x)
     for x in range(4):
         lift_inner(x)
     for x in range(0, 16, 2):
+        if x == 14:
+            for copy in y_copies:
+                copy.wait_recv()
+            for h in range(8):
+                lay_outer(h)
+            for h in range(6):
+                lift_outer(h)
         for h in range(2):
+            if x + 6 + h < 20:
+                lay_inner(x + 6 + h)
             if x + 4 + h < 18:
                 lift_inner(x + 4 + h)
-        encode(x, 2, ((64, 224),))
-    for copy in y_copies:
-        copy.wait_recv()
-    for x in range(20):
-        lay_outer(x)
-    for x in range(6):
-        lift_outer(x)
+        encode(x, 1, ((64, 224),))
+        encode(x + 1, 1, ((64, 224),))
     for x in range(0, 16, 4):
         for h in range(4):
+            if x + 8 + h < 20:
+                lay_outer(x + 8 + h)
             if x + 6 + h < 18:
                 lift_outer(x + 6 + h)
-        encode(x, 4, ((0, 64), (288, 64)))
+        encode(x, 2, ((0, 64), (288, 64)))
+        encode(x + 2, 2, ((0, 64), (288, 64)))
         if x:
             downward(x // 2 - 2)
             downward(x // 2 - 1)
@@ -377,35 +390,38 @@
             if (f + 1) // 2 == x - 1:
                 upsample(f)
     upsample(5)
-    decode(0, 2)
-    decode(2, 2)
-
-    h = heads[...].reshape(64, 128)
-    coarse_part = h.astype(BF)
-    total = jnp.zeros((192, 32), F32)
-    for part in (coarse_part, (h - coarse_part.astype(F32)).astype(BF)):
-        for jy in range(2):
-            t = lax.dot_general(rows[jy], part, (((0,), (0,)), ((), ())), preferred_element_type=F32)
-            t = jnp.where(keep, t, 0.0).astype(BF)
-            total = total + lax.dot_general(
-                t, place[:, 128 * jy : 128 * jy + 128], (((1,), (1,)), ((), ())), preferred_element_type=F32
-            )
-    out[...] = total.reshape(3, 4, 16, 32)
+    v = jnp.concatenate([decode(x, 1) for x in range(4)], axis=0)
+
+    h = lax.dot_general(whs[...], v, (((1,), (1,)), ((), ())), preferred_element_type=F32)
+    spot = lax.broadcasted_iota(jnp.int32, (96, 512), 0) % 16 // 2 == lax.broadcasted_iota(jnp.int32, (96, 512), 1) % 8
+    h = jnp.where(spot, h, 0.0)
+    rough = h.astype(BF)
+    fine = (h - rough.astype(F32)).astype(BF)
+    sums = []
+    for part in (rough, fine):
+        wide_part = jnp.concatenate([
+            jnp.concatenate([part[48 * jy : 48 * jy + 48, 128 * x : 128 * x + 128] for x in range(4)], axis=0)
+            for jy in range(2)
+        ], axis=1)
+        sums.append(lax.dot_general(wide_part, place[...], (((1,), (1,)), ((), ())), preferred_element_type=F32))
+    total = (sums[0] + sums[1]).reshape(4, 3, 16, 32)
+    for x in range(4):
+        out[:, x] = total[x]
     for copy in x_copies + z_copies + y_copies:
         copy.wait_send()
 
 
 def local(d, lw, ew, dw, m1, m2, uw, cw, hw):
-    anywhere = pl.BlockSpec(memory_space=pl.ANY)
+    anywhere = pl.BlockSpec(memory_space=pltpu.HBM)
     args = (
         jnp.transpose(d, (0, 1, 3, 2)), jnp.asarray(place_columns(), BF), jnp.asarray(gather_rows(), BF),
         jnp.transpose(lw, (2, 0, 1)), jnp.asarray(lift_selection(), BF), ew, cw, jnp.asarray(widen_lanes(), BF),
-        m1, m2, uw, jnp.transpose(dw, (0, 2, 1)), hw,
+        m1, m2, uw, jnp.transpose(dw, (0, 2, 1)), hw, jnp.asarray(spread_head(), BF),
     )
     out = pl.pallas_call(
         unet,
         out_shape=jax.ShapeDtypeStruct((3, 4, 16, 32), F32),
-        in_specs=[anywhere] * 13,
+        in_specs=[anywhere] * 14,
         out_specs=pl.BlockSpec(memory_space=pltpu.VMEM),
         scratch_shapes=[pltpu.VMEM(arg.shape, arg.dtype) for arg in args] + [
             pltpu.VMEM((20, 16, 128), BF),
@@ -414,7 +430,7 @@
             pltpu.VMEM((2, 10, 16, 128), BF),
             pltpu.VMEM((2, 10, 16, 128), BF),
             pltpu.VMEM((320, 384), BF),
-            pltpu.VMEM((4, 16, 128), F32),
+            pltpu.VMEM((96, 256), BF),
             pltpu.VMEM((20, 16, 256), F32),
             pltpu.VMEM((20, 64, 256), BF),
             pltpu.VMEM((20, 64, 128), BF),
@@ -434,7 +450,7 @@
             pltpu.VMEM((4, 144, 256), BF),
             pltpu.VMEM((2, 2, 6, 128, 256), BF),
             pltpu.VMEM((2, 2, 6, 128, 256), BF),
-            pltpu.SemaphoreType.DMA((13,)),
+            pltpu.SemaphoreType.DMA((14,)),
             pltpu.SemaphoreType.DMA((4,)),
             pltpu.SemaphoreType.DMA((4,)),
             pltpu.SemaphoreType.DMA((2,)),

time: 39.5 us -> 37.3 us (0.944)
  Pallas kernels: 37.8 us -> 35.6 us
    pallas_call x1, Pallas kernels: 37.8 us -> 35.6 us  [local(): pl.pallas_call(unet, out_shape=jax.ShapeDtypeStruct((3, 4, 16, 32), F32),...]
where the time goes in v4:
time: 37.3 us; the launch traced here: 37.2 us
  Pallas kernels  35.6 us (95%)
  other arithmetic  1.54 us (4%)
    pallas_call x1, Pallas kernels, local(): pl.pallas_call(unet, out_shape=jax.ShapeDtypeStruct((3, 4, 16, 32), F32),...  35.6 us
    add x1, other arithmetic, local(): return d.astype(F32) + jnp.transpose(out, (0, 1, 3, 2))  1.54 us

profile of v4, /device:TPU:1, one launch (start us, length us, event | category | flops | bytes accessed | tf_op | source)
XLA Modules:
  0.0 37.2 jit_solution(4824033130626400641)
XLA Ops:
  0.0 0.0 copy-start
  0.0 35.6 %shard_map.136 = f32[3,4,16,32]{3,2,1,0:T(8,128)} custom-call(bf16[3,4,16,32]{3,2,1,0:T(8,128)(2,1)} %bitcast.5, bf16[32,256]{1,0:T(8,128)(2,1)} %constant.10.clone.place_hbm, bf16[2,64,192]{2,1,0:T(8,128)(2,1)} %constant.11.clone.rows_hbm, bf16[3,27,64]{2,1,0:T(8,128)(2,1)} %bitcast.7, bf16[3,768,27]{2,1,0:T(8,128)(2,1)} %constant.12.clone.sel_hbm, ...), custom_call_target="tpu_custom_call" | custom-call | tf_op jit(solution)/shard_map/pallas_call | solution.py:421
  35.6 0.0 copy-done
  35.6 1.5 %bitcast_add_fusion = f32[3,4,32,16]{2,3,1,0:T(8,128)} fusion(f32[3,4,16,32]{3,2,1,0:T(8,128)} %shard_map.136, bf16[3,4,32,16]{2,3,1,0:T(8,128)(2,1)S(1)} %copy-done), kind=kLoop, calls=%fused_computation | loop fusion | flops 12288 | bytes 61440 | tf_op jit(solution)/shard_map/add | solution.py:465
Async XLA Ops:
  0.0 35.6 %copy-start = (bf16[3,4,32,16]{2,3,1,0:T(8,128)(2,1)S(1)}, bf16[3,4,32,16]{2,3,1,0:T(8,128)(2,1)}, u32[]{:S(2)}) copy-start(bf16[3,4,32,16]{2,3,1,0:T(8,128)(2,1)} %param.14) | copy-start | bytes 36868

commit v5 on v4

--- a/solution.py
+++ b/solution.py
@@ -420,7 +420,7 @@
     )
     out = pl.pallas_call(
         unet,
-        out_shape=jax.ShapeDtypeStruct((3, 4, 16, 32), F32),
+        out_shape=pltpu.VMEM((3, 4, 16, 32), F32),
         in_specs=[anywhere] * 14,
         out_specs=pl.BlockSpec(memory_space=pltpu.VMEM),
         scratch_shapes=[pltpu.VMEM(arg.shape, arg.dtype) for arg in args] + [

time: 37.3 us -> 35.7 us (0.957)
  other arithmetic: 1.54 us -> 0.65 us
  Pallas kernels: 35.6 us -> 35 us
    add x1, other arithmetic: 1.54 us -> 0.65 us  [local(): return d.astype(F32) + jnp.transpose(out, (0, 1, 3, 2))]
    pallas_call x1, Pallas kernels: 35.6 us -> 35 us  [local(): pl.pallas_call(unet, out_shape=pltpu.VMEM((3, 4, 16, 32), F32), in_specs=...]
where the time goes in v5:
time: 35.7 us
  Pallas kernels  35 us (98%)
  other arithmetic  0.65 us (2%)
    pallas_call x1, Pallas kernels, local(): pl.pallas_call(unet, out_shape=pltpu.VMEM((3, 4, 16, 32), F32), in_specs=...  35 us

profile of v5, /device:TPU:1, one launch (start us, length us, event | category | flops | bytes accessed | tf_op | source)
XLA Modules:
  0.0 35.7 jit_solution(7566364642745028130)
XLA Ops:
  0.0 0.0 copy-start
  0.0 35.0 %shard_map.136 = f32[3,4,16,32]{3,2,1,0:T(8,128)S(1)} custom-call(bf16[3,4,16,32]{3,2,1,0:T(8,128)(2,1)} %bitcast.5, bf16[32,256]{1,0:T(8,128)(2,1)} %constant.10.clone.place_hbm, bf16[2,64,192]{2,1,0:T(8,128)(2,1)} %constant.11.clone.rows_hbm, bf16[3,27,64]{2,1,0:T(8,128)(2,1)} %bitcast.7, bf16[3,768,27]{2,1,0:T(8,128)(2,1)} %constant.12.clone.sel_hbm, ...), custom_call_target="tpu_custom_call" | custom-call | tf_op jit(solution)/shard_map/pallas_call | solution.py:421
  35.0 0.0 copy-done
  35.0 0.7 %bitcast_add_fusion = f32[3,4,32,16]{2,3,1,0:T(8,128)} fusion(f32[3,4,16,32]{3,2,1,0:T(8,128)S(1)} %shard_map.136, bf16[3,4,32,16]{2,3,1,0:T(8,128)(2,1)S(1)} %copy-done), kind=kLoop, calls=%fused_computation | loop fusion | flops 12288 | bytes 61440 | tf_op jit(solution)/shard_map/add | solution.py:465
Async XLA Ops:
  0.0 35.0 %copy-start = (bf16[3,4,32,16]{2,3,1,0:T(8,128)(2,1)S(1)}, bf16[3,4,32,16]{2,3,1,0:T(8,128)(2,1)}, u32[]{:S(2)}) copy-start(bf16[3,4,32,16]{2,3,1,0:T(8,128)(2,1)} %param.14) | copy-start | bytes 36868

commit v6 on v5

--- a/solution.py
+++ b/solution.py
@@ -60,10 +60,11 @@
 
 def widen_lanes():
     wide = np.zeros((384, 256), np.float32)
-    for piece, (first, last, shift) in enumerate(((0, 8, 4), (4, 8, -4), (0, 4, 12))):
-        for z in range(first, last):
-            for y in range(16):
-                wide[128 * piece + 8 * y + z, 16 * y + z + shift] = 1
+    for z in range(8):
+        for y in range(16):
+            wide[8 * y + z, 16 * y + z + 4] = 1
+            wide[128 + 8 * y + z, 16 * y + z % 4] = 1
+            wide[256 + 8 * y + z, 16 * y + 12 + z % 4] = 1
     return wide
 
 
@@ -83,7 +84,7 @@
     m1_hbm, m2_hbm, uw_hbm, dw_hbm, hw_hbm, spr_hbm,
     out,
     disp, place, rows, lw, sel, ew, cw, wide, m1, m2, uw, dw, hw, spr,
-    layers, left, right, slab_out, slab_in, sides, whs, mid,
+    layers, packs, left, right, slab_out, slab_in, sides, whs, mid,
     patch, edge, wl, we, wd, wm1, wm2, wu, wc, wh,
     f0, f1, skip, coarse, middle, deep, ks, ku,
     load_sem, x_send, x_recv, z_send, z_recv, y_send, y_recv,
@@ -97,12 +98,13 @@
     def at_y(step):
         return {"gy": lax.rem(gy + ny + step, ny)}
 
-    def at_z(step):
-        return {"gz": lax.rem(gz + nz + step, nz)}
+    def at_xz(step, turn):
+        return {"gx": lax.rem(gx + nx + step, nx), "gz": lax.rem(gz + nz + turn, nz)}
 
     steps = (-2, -1, 1, 2)
     barrier = pltpu.get_barrier_semaphore()
-    for where in [at_x(step) for step in steps] + [at_y(-1), at_y(1), at_z(-1), at_z(1)]:
+    sideways = [(step, turn) for turn in (1, -1) for step in (-2, 2, -1, 1, 0)]
+    for where in [at_x(step) for step in steps] + [at_xz(*move) for move in sideways] + [at_y(-1), at_y(1)]:
         pl.semaphore_signal(barrier, inc=1, device_id=where, device_id_type=pl.DeviceIdType.MESH)
 
     loads = [
@@ -127,14 +129,24 @@
         part = jnp.where(keep, cells[:, 128 * jy : 128 * jy + 128], 0.0).astype(BF)
         own = own + dot(rows[jy], part)
     layers[8:12] = own.astype(BF).reshape(4, 16, 128)
-
-    pl.semaphore_wait(barrier, 8)
-    x_copies = []
+    first_four = lax.broadcasted_iota(jnp.int32, (2, 16, 128), 2) % 8 < 4
+    even, odd = own.reshape(2, 2, 16, 128)[:, 0], own.reshape(2, 2, 16, 128)[:, 1]
+    packs[0] = jnp.where(first_four, pltpu.roll(even, 124, axis=2), odd).astype(BF)
+    packs[1] = jnp.where(first_four, even, pltpu.roll(odd, 4, axis=2)).astype(BF)
+
+    pl.semaphore_wait(barrier, 16)
+    x_copies, z_copies = [], []
     for n, step in enumerate(steps):
         x_copies.append(remote(
             layers.at[8:12], layers.at[pl.ds(8 - 4 * step, 4)], x_send.at[n], x_recv.at[n], **at_x(step)
         ))
-        x_copies[-1].start()
+    for n, (step, turn) in enumerate(sideways):
+        src, dst = (packs.at[0], left) if turn == 1 else (packs.at[1], right)
+        z_copies.append(remote(
+            src, dst.at[pl.ds(4 - 2 * step, 2)], z_send.at[n], z_recv.at[n], **at_xz(step, turn)
+        ))
+    for copy in z_copies + x_copies:
+        copy.start()
 
     for load in loads[3:7]:
         load.wait()
@@ -172,15 +184,6 @@
                             for s in range(2):
                                 row = (((s * 3 + a) * 2 + dy) * 2 + dz) * 256 + (jy * 2 + jz) * 64
                                 wc[row : row + 64, oy * 128 : oy * 128 + 128] = tile[s * 64 : s * 64 + 64]
-
-    for copy in x_copies:
-        copy.wait_recv()
-    z_copies = [
-        remote(layers, left, z_send.at[0], z_recv.at[0], **at_z(1)),
-        remote(layers, right, z_send.at[1], z_recv.at[1], **at_z(-1)),
-    ]
-    for copy in z_copies:
-        copy.start()
 
     for load in loads[7:]:
         load.wait()
@@ -207,10 +210,14 @@
         wh[3 * g : 3 * g + 3, 64 * g : 64 * g + 64] = hw[...].astype(F32)
     whs[...] = dot(spr[...], wh[...].astype(BF)).astype(BF)
 
-    for copy in z_copies:
+    for copy in x_copies + z_copies:
         copy.wait_recv()
-    for n, src in enumerate((layers, left, right)):
-        sides[:, 128 * n : 128 * n + 128] = src[...].reshape(320, 128)
+    first_four = lax.broadcasted_iota(jnp.int32, (10, 16, 128), 2) % 8 < 4
+    sides[:, 0:128] = layers[...].reshape(320, 128)
+    for n, src in ((1, left), (2, right)):
+        pack = src[...].astype(F32)
+        split = jnp.stack([jnp.where(first_four, pack, 0.0), jnp.where(first_four, 0.0, pack)], axis=1)
+        sides[:, 128 * n : 128 * n + 128] = split.reshape(320, 128).astype(BF)
     mid[...] = dot(sides[...], wide[...]).reshape(20, 16, 256)
     half = lax.broadcasted_iota(jnp.int32, (10, 16, 128), 2) < 64
     pairs = mid[...].reshape(10, 2, 16, 256)
@@ -338,42 +345,42 @@
             halves.append(jnp.where(low, s, pltpu.roll(s, 15, axis=1)))
         spread(ku, f, jnp.concatenate(halves, axis=2))
 
-    def decode(x, n):
+    def decode(x):
         taps = []
         for src in (ks, ku):
             for a in range(3):
                 for dy in range(2):
                     for dz in range(2):
-                        taps.append(src[dy, dz, x + a : x + a + n].reshape(128 * n, 256))
+                        taps.append(src[dy, dz, x + a])
         return act(dot(jnp.concatenate(taps, axis=1), wc[...])).astype(BF)
 
     for x in range(6):
         lay_inner(x)
     for x in range(4):
         lift_inner(x)
-    for x in range(0, 16, 2):
-        if x == 14:
-            for copy in y_copies:
-                copy.wait_recv()
-            for h in range(8):
-                lay_outer(h)
-            for h in range(6):
-                lift_outer(h)
+    inner, both_ends = ((64, 224),), ((0, 64), (288, 64))
+    for x in range(0, 14, 2):
         for h in range(2):
-            if x + 6 + h < 20:
-                lay_inner(x + 6 + h)
-            if x + 4 + h < 18:
-                lift_inner(x + 4 + h)
-        encode(x, 1, ((64, 224),))
-        encode(x + 1, 1, ((64, 224),))
+            lay_inner(x + 6 + h)
+            lift_inner(x + 4 + h)
+        encode(x, 1, inner)
+        encode(x + 1, 1, inner)
+    for copy in y_copies:
+        copy.wait_recv()
+    for x in range(10):
+        lay_outer(x)
+    encode(14, 1, inner)
+    for x in range(6):
+        lift_outer(x)
+    encode(15, 1, inner)
     for x in range(0, 16, 4):
         for h in range(4):
-            if x + 8 + h < 20:
-                lay_outer(x + 8 + h)
+            if x + 10 + h < 20:
+                lay_outer(x + 10 + h)
             if x + 6 + h < 18:
                 lift_outer(x + 6 + h)
-        encode(x, 2, ((0, 64), (288, 64)))
-        encode(x + 2, 2, ((0, 64), (288, 64)))
+        encode(x, 2, both_ends)
+        encode(x + 2, 2, both_ends)
         if x:
             downward(x // 2 - 2)
             downward(x // 2 - 1)
@@ -390,7 +397,7 @@
             if (f + 1) // 2 == x - 1:
                 upsample(f)
     upsample(5)
-    v = jnp.concatenate([decode(x, 1) for x in range(4)], axis=0)
+    v = jnp.concatenate([decode(x) for x in range(4)], axis=0)
 
     h = lax.dot_general(whs[...], v, (((1,), (1,)), ((), ())), preferred_element_type=F32)
     spot = lax.broadcasted_iota(jnp.int32, (96, 512), 0) % 16 // 2 == lax.broadcasted_iota(jnp.int32, (96, 512), 1) % 8
@@ -425,8 +432,9 @@
         out_specs=pl.BlockSpec(memory_space=pltpu.VMEM),
         scratch_shapes=[pltpu.VMEM(arg.shape, arg.dtype) for arg in args] + [
             pltpu.VMEM((20, 16, 128), BF),
-            pltpu.VMEM((20, 16, 128), BF),
-            pltpu.VMEM((20, 16, 128), BF),
+            pltpu.VMEM((2, 2, 16, 128), BF),
+            pltpu.VMEM((10, 16, 128), BF),
+            pltpu.VMEM((10, 16, 128), BF),
             pltpu.VMEM((2, 10, 16, 128), BF),
             pltpu.VMEM((2, 10, 16, 128), BF),
             pltpu.VMEM((320, 384), BF),
@@ -453,8 +461,8 @@
             pltpu.SemaphoreType.DMA((14,)),
             pltpu.SemaphoreType.DMA((4,)),
             pltpu.SemaphoreType.DMA((4,)),
-            pltpu.SemaphoreType.DMA((2,)),
-            pltpu.SemaphoreType.DMA((2,)),
+            pltpu.SemaphoreType.DMA((10,)),
+            pltpu.SemaphoreType.DMA((10,)),
             pltpu.SemaphoreType.DMA((2,)),
             pltpu.SemaphoreType.DMA((2,)),
         ],

time: 35.7 us -> 33.3 us (0.933)
  Pallas kernels: 35 us -> 32.6 us
    pallas_call x1, Pallas kernels: 35 us -> 32.6 us  [local(): pl.pallas_call(unet, out_shape=pltpu.VMEM((3, 4, 16, 32), F32), in_specs=...]
where the time goes in v6:
time: 33.3 us; the launch traced here: 33.2 us
  Pallas kernels  32.6 us (98%)
  other arithmetic  0.65 us (2%)
    pallas_call x1, Pallas kernels, local(): pl.pallas_call(unet, out_shape=pltpu.VMEM((3, 4, 16, 32), F32), in_specs=...  32.6 us

profile of v6, /device:TPU:1, one launch (start us, length us, event | category | flops | bytes accessed | tf_op | source)
XLA Modules:
  0.0 33.2 jit_solution(14205405302026042782)
XLA Ops:
  0.0 0.0 copy-start
  0.0 32.6 %shard_map.136 = f32[3,4,16,32]{3,2,1,0:T(8,128)S(1)} custom-call(bf16[3,4,16,32]{3,2,1,0:T(8,128)(2,1)} %bitcast.5, bf16[32,256]{1,0:T(8,128)(2,1)} %constant.10.clone.place_hbm, bf16[2,64,192]{2,1,0:T(8,128)(2,1)} %constant.11.clone.rows_hbm, bf16[3,27,64]{2,1,0:T(8,128)(2,1)} %bitcast.7, bf16[3,768,27]{2,1,0:T(8,128)(2,1)} %constant.12.clone.sel_hbm, ...), custom_call_target="tpu_custom_call" | custom-call | tf_op jit(solution)/shard_map/pallas_call | solution.py:428
  32.6 0.0 copy-done
  32.6 0.7 %bitcast_add_fusion = f32[3,4,32,16]{2,3,1,0:T(8,128)} fusion(f32[3,4,16,32]{3,2,1,0:T(8,128)S(1)} %shard_map.136, bf16[3,4,32,16]{2,3,1,0:T(8,128)(2,1)S(1)} %copy-done), kind=kLoop, calls=%fused_computation | loop fusion | flops 12288 | bytes 61440 | tf_op jit(solution)/shard_map/add | solution.py:473
Async XLA Ops:
  0.0 32.6 %copy-start = (bf16[3,4,32,16]{2,3,1,0:T(8,128)(2,1)S(1)}, bf16[3,4,32,16]{2,3,1,0:T(8,128)(2,1)}, u32[]{:S(2)}) copy-start(bf16[3,4,32,16]{2,3,1,0:T(8,128)(2,1)} %param.14) | copy-start | bytes 36868

commit v7 on v6

--- a/solution.py
+++ b/solution.py
@@ -115,10 +115,12 @@
             (m1_hbm, m1), (m2_hbm, m2), (uw_hbm, uw), (dw_hbm, dw), (hw_hbm, hw), (spr_hbm, spr),
         ))
     ]
-    for load in loads:
+    for load in loads[:3]:
         load.start()
     for load in loads[:3]:
         load.wait()
+    for load in loads[3:]:
+        load.start()
 
     row_z = lax.broadcasted_iota(jnp.int32, (192, 128), 0) % 16 // 2
     lane_z = lax.broadcasted_iota(jnp.int32, (192, 128), 1) % 8
@@ -218,20 +220,8 @@
         pack = src[...].astype(F32)
         split = jnp.stack([jnp.where(first_four, pack, 0.0), jnp.where(first_four, 0.0, pack)], axis=1)
         sides[:, 128 * n : 128 * n + 128] = split.reshape(320, 128).astype(BF)
-    mid[...] = dot(sides[...], wide[...]).reshape(20, 16, 256)
-    half = lax.broadcasted_iota(jnp.int32, (10, 16, 128), 2) < 64
-    pairs = mid[...].reshape(10, 2, 16, 256)
-    upper = jnp.where(half, pltpu.roll(pairs[:, 0, :, 128:], 64, axis=2), pairs[:, 1, :, 128:])
-    lower = jnp.where(half, pairs[:, 0, :, :128], pltpu.roll(pairs[:, 1, :, :128], 64, axis=2))
-    slab_out[0] = upper.astype(BF)
-    slab_out[1] = lower.astype(BF)
-    y_copies = [
-        remote(slab_out.at[0], slab_in.at[0], y_send.at[0], y_recv.at[0], **at_y(1)),
-        remote(slab_out.at[1], slab_in.at[1], y_send.at[1], y_recv.at[1], **at_y(-1)),
-    ]
-    for copy in y_copies:
-        copy.start()
-
+    for n in range(2):
+        mid[10 * n : 10 * n + 10] = dot(sides[160 * n : 160 * n + 160], wide[...]).reshape(10, 16, 256)
     def lay_inner(x):
         q = mid[x]
         for dy in range(2):
@@ -358,8 +348,21 @@
         lay_inner(x)
     for x in range(4):
         lift_inner(x)
+    half = lax.broadcasted_iota(jnp.int32, (10, 16, 128), 2) < 64
+    pairs = mid[...].reshape(10, 2, 16, 256)
+    upper = jnp.where(half, pltpu.roll(pairs[:, 0, :, 128:], 64, axis=2), pairs[:, 1, :, 128:])
+    lower = jnp.where(half, pairs[:, 0, :, :128], pltpu.roll(pairs[:, 1, :, :128], 64, axis=2))
+    slab_out[0] = upper.astype(BF)
+    slab_out[1] = lower.astype(BF)
+    y_copies = [
+        remote(slab_out.at[0], slab_in.at[0], y_send.at[0], y_recv.at[0], **at_y(1)),
+        remote(slab_out.at[1], slab_in.at[1], y_send.at[1], y_recv.at[1], **at_y(-1)),
+    ]
+    for copy in y_copies:
+        copy.start()
+
     inner, both_ends = ((64, 224),), ((0, 64), (288, 64))
-    for x in range(0, 14, 2):
+    for x in range(0, 12, 2):
         for h in range(2):
             lay_inner(x + 6 + h)
             lift_inner(x + 4 + h)
@@ -367,8 +370,14 @@
         encode(x + 1, 1, inner)
     for copy in y_copies:
         copy.wait_recv()
+    for x in range(18, 20):
+        lay_inner(x)
+    for x in range(16, 18):
+        lift_inner(x)
+    encode(12, 1, inner)
     for x in range(10):
         lay_outer(x)
+    encode(13, 1, inner)
     encode(14, 1, inner)
     for x in range(6):
         lift_outer(x)

time: 33.3 us -> 33.1 us (level)
  no operation moved by 1% of the time
where the time goes in v7:
time: 33.1 us; the launch traced here: 33 us
  Pallas kernels  32.3 us (98%)
  other arithmetic  0.65 us (2%)
    pallas_call x1, Pallas kernels, local(): pl.pallas_call(unet, out_shape=pltpu.VMEM((3, 4, 16, 32), F32), in_specs=...  32.3 us

profile of v7, /device:TPU:1, one launch (start us, length us, event | category | flops | bytes accessed | tf_op | source)
XLA Modules:
  0.0 33.0 jit_solution(16383368015463079643)
XLA Ops:
  0.0 0.0 copy-start
  0.0 32.3 %shard_map.136 = f32[3,4,16,32]{3,2,1,0:T(8,128)S(1)} custom-call(bf16[3,4,16,32]{3,2,1,0:T(8,128)(2,1)} %bitcast.5, bf16[32,256]{1,0:T(8,128)(2,1)} %constant.10.clone.place_hbm, bf16[2,64,192]{2,1,0:T(8,128)(2,1)} %constant.11.clone.rows_hbm, bf16[3,27,64]{2,1,0:T(8,128)(2,1)} %bitcast.7, bf16[3,768,27]{2,1,0:T(8,128)(2,1)} %constant.12.clone.sel_hbm, ...), custom_call_target="tpu_custom_call" | custom-call | tf_op jit(solution)/shard_map/pallas_call | solution.py:437
  32.3 0.0 copy-done
  32.3 0.7 %bitcast_add_fusion = f32[3,4,32,16]{2,3,1,0:T(8,128)} fusion(f32[3,4,16,32]{3,2,1,0:T(8,128)S(1)} %shard_map.136, bf16[3,4,32,16]{2,3,1,0:T(8,128)(2,1)S(1)} %copy-done), kind=kLoop, calls=%fused_computation | loop fusion | flops 12288 | bytes 61440 | tf_op jit(solution)/shard_map/add | solution.py:482
Async XLA Ops:
  0.0 32.3 %copy-start = (bf16[3,4,32,16]{2,3,1,0:T(8,128)(2,1)S(1)}, bf16[3,4,32,16]{2,3,1,0:T(8,128)(2,1)}, u32[]{:S(2)}) copy-start(bf16[3,4,32,16]{2,3,1,0:T(8,128)(2,1)} %param.14) | copy-start | bytes 36868

commit v8 on v7

--- a/solution.py
+++ b/solution.py
@@ -147,7 +147,8 @@
         z_copies.append(remote(
             src, dst.at[pl.ds(4 - 2 * step, 2)], z_send.at[n], z_recv.at[n], **at_xz(step, turn)
         ))
-    for copy in z_copies + x_copies:
+    far, near = [x_copies[0], x_copies[3]], x_copies[1:3]
+    for copy in far + z_copies[0:2] + z_copies[5:7] + near + z_copies[2:5] + z_copies[7:10]:
         copy.start()
 
     for load in loads[3:7]:

time: 33.1 us -> 33.4 us (level)
  no operation moved by 1% of the time
where the time goes in v8:
time: 33.4 us; the launch traced here: 33.3 us
  Pallas kernels  32.6 us (98%)
  other arithmetic  0.65 us (2%)
    pallas_call x1, Pallas kernels, local(): pl.pallas_call(unet, out_shape=pltpu.VMEM((3, 4, 16, 32), F32), in_specs=...  32.6 us

profile of v8, /device:TPU:1, one launch (start us, length us, event | category | flops | bytes accessed | tf_op | source)
XLA Modules:
  0.0 33.3 jit_solution(9046597117996384893)
XLA Ops:
  0.0 0.0 copy-start
  0.0 32.6 %shard_map.136 = f32[3,4,16,32]{3,2,1,0:T(8,128)S(1)} custom-call(bf16[3,4,16,32]{3,2,1,0:T(8,128)(2,1)} %bitcast.5, bf16[32,256]{1,0:T(8,128)(2,1)} %constant.10.clone.place_hbm, bf16[2,64,192]{2,1,0:T(8,128)(2,1)} %constant.11.clone.rows_hbm, bf16[3,27,64]{2,1,0:T(8,128)(2,1)} %bitcast.7, bf16[3,768,27]{2,1,0:T(8,128)(2,1)} %constant.12.clone.sel_hbm, ...), custom_call_target="tpu_custom_call" | custom-call | tf_op jit(solution)/shard_map/pallas_call | solution.py:438
  32.6 0.0 copy-done
  32.6 0.7 %bitcast_add_fusion = f32[3,4,32,16]{2,3,1,0:T(8,128)} fusion(f32[3,4,16,32]{3,2,1,0:T(8,128)S(1)} %shard_map.136, bf16[3,4,32,16]{2,3,1,0:T(8,128)(2,1)S(1)} %copy-done), kind=kLoop, calls=%fused_computation | loop fusion | flops 12288 | bytes 61440 | tf_op jit(solution)/shard_map/add | solution.py:483
Async XLA Ops:
  0.0 32.6 %copy-start = (bf16[3,4,32,16]{2,3,1,0:T(8,128)(2,1)S(1)}, bf16[3,4,32,16]{2,3,1,0:T(8,128)(2,1)}, u32[]{:S(2)}) copy-start(bf16[3,4,32,16]{2,3,1,0:T(8,128)(2,1)} %param.14) | copy-start | bytes 36868
